TPU v7x, 256 devices: a whole 4x4x8 slice. The times are simulated.
256 devices in a mesh: section: 4 (over y), fsdp: 64 (over z, x, core).
Axes of the slice: x: 4, y: 4, z: 8, core: 2. Of those that a mesh axis runs over, the one named last changes fastest.
Arguments:
- residual_input: bfloat16 [2, 4096, 8192], P(None, 'fsdp'), may hold values from -16 to 16
- output_gradient: bfloat16 [2, 4096, 8192], P(None, 'fsdp'), may hold values from -0.0068359375 to 0.0068359375
- value_projection_weight: bfloat16 [4, 8192, 512], P('section', 'fsdp'), may hold values from -0.0625 to 0.0625
- output_weight: bfloat16 [4, 512, 8192], P('section', None, 'fsdp'), may hold values from -0.25 to 0.25
- adapter_down_weight: bfloat16 [4, 8192, 160], P('section'), may hold values from -0.0625 to 0.0625
- adapter_up_weight: bfloat16 [4, 160, 512], P('section'), may hold values from -0.625 to 0.625
- input_norm_scale: float32 [4, 8192], P('section'), may hold values from 0.25 to 1.75
- segment_adapter_index: int32 [2, 128], P(None, 'fsdp'), may hold values from 0 to 3
- adapter_rank_blocks: int32 [4], replicated, may hold values from 1 to 16, 20 in all
Outputs:
- grad_down: float32 [4, 8192, 160], P('section', 'fsdp')
- grad_up: float32 [4, 160, 512], P('section', None, 'fsdp')
Inputs may be any that keep to these rules, and one draw needn't show every extreme that they name: `segment_adapter_index`: adapter of each block of 32 consecutive tokens. `adapter_rank_blocks`: the entries sum to 20.
All inputs are finite; a program needn't handle non-finite values.
Results may differ from a plain program's by a relative error of at most 0.014.
Values may be sent and summed in bfloat16 or wider, within the bound.
No kernel may reach another device: no remote copies, remote signals or barrier semaphores. Data moves between devices by JAX's collectives and lax.ppermute only.
A program may use at most 128 MiB of HBM per device.

v0:
```python
import jax
import jax.numpy as jnp
from jax import lax
from jax.experimental.layout import Layout, with_layout_constraint
from jax.sharding import Mesh, PartitionSpec as P

ADAPTERS = 4
EPSILON = 1e-06
ADAPTER_ALPHA = 32.0
BF = jnp.bfloat16
F32 = jnp.float32
GROUP = ("y", "z", "c")


def contract(left, right, left_dim, right_dim):
    return lax.dot_general(
        left, right, (((left_dim,), (right_dim,)), ((), ())), preferred_element_type=F32
    )


def split_pair(value):
    high = lax.reduce_precision(value, 8, 7)
    return high.astype(BF), (value - high).astype(BF)


def coefficient_row(adapter, adapter_rank_blocks, columns):
    rank_sizes = 8 * adapter_rank_blocks
    adapters = jnp.arange(ADAPTERS, dtype=jnp.int32)
    ends = jnp.sum(
        jnp.where(adapters[None, :] <= adapters[:, None], rank_sizes[None, :], 0), axis=1
    )
    column = jnp.arange(columns, dtype=jnp.int32)
    owner = jnp.sum((column[:, None] >= ends[None, :]).astype(jnp.int32), axis=1)
    rank = jnp.sum(jnp.where(adapters == adapter, rank_sizes, 0)).astype(F32)
    return jnp.where(owner == adapter, ADAPTER_ALPHA / rank, 0.0)[None, :]


def exchanged(value, axis):
    return lax.all_to_all(value, axis, split_axis=0, concat_axis=0, tiled=True)


def summed(value):
    return value.astype(F32).sum(axis=0)


def gathered_sum(partial):
    return summed(lax.all_gather(partial, "x", axis=0, tiled=False))


def local(
    residual_input,
    output_gradient,
    value_projection_weight,
    output_weight,
    adapter_down_weight,
    adapter_up_weight,
    input_norm_scale,
    segment_adapter_index,
    adapter_rank_blocks,
):
    ny, nz, nx, nc = (lax.axis_size(name) for name in ("y", "z", "x", "c"))
    yi, zi, xi, ci = (lax.axis_index(name) for name in ("y", "z", "x", "c"))
    rows = value_projection_weight.shape[1]
    value_cols = value_projection_weight.shape[2]
    packed = adapter_down_weight.shape[2]
    width = adapter_down_weight.shape[1]
    both = value_cols + packed
    layers = ny
    lanes = nc * rows
    depth = nz * lanes

    joined = jnp.concatenate([value_projection_weight[0], output_weight[0].T], axis=1)
    joined = with_layout_constraint(joined, Layout(major_to_minor=(0, 1)))
    full = lax.all_gather(joined, GROUP, axis=0, tiled=False)
    full = with_layout_constraint(full, Layout(major_to_minor=(0, 1, 2)))
    full = full.reshape(layers, depth, 2 * value_cols)
    value_full = [full[layer, :, :value_cols] for layer in range(layers)]
    out_full = [full[layer, :, value_cols:] for layer in range(layers)]

    all_tokens = residual_input.shape[0] * residual_input.shape[1]
    tokens = all_tokens // ny
    first = yi * tokens
    own = jnp.stack(
        [
            lax.dynamic_slice(array.reshape(all_tokens, width), (first, 0), (tokens, width))
            for array in (residual_input, output_gradient)
        ]
    )
    own = own.reshape(2, tokens, nz, nx, lanes).transpose(3, 0, 1, 2, 4)
    spread = exchanged(own.reshape(nx, 2, tokens, depth), "x")
    state = spread[:, 0].reshape(nx * tokens, depth)
    grad = spread[:, 1].reshape(nx * tokens, depth)

    down_local = lax.dynamic_index_in_dim(
        adapter_down_weight[0].T.reshape(packed, nz, nx, lanes), xi, 2, keepdims=False
    ).reshape(1, packed, depth)
    downs_full = exchanged(jnp.broadcast_to(down_local, (layers, packed, depth)), "y")

    gains_local = lax.dynamic_index_in_dim(
        input_norm_scale.reshape(nz, nx, lanes), xi, 1, keepdims=False
    ).reshape(depth)
    gains = lax.all_gather(gains_local, "y", axis=0, tiled=False)
    ups = lax.all_gather(adapter_up_weight[0], "y", axis=0, tiled=False)
    adapter = lax.dynamic_index_in_dim(segment_adapter_index.reshape(ny), yi, 0, keepdims=False)
    coef_row = coefficient_row(adapter, adapter_rank_blocks, packed)
    coef = lax.all_gather(
        jnp.broadcast_to(coef_row, (tokens, packed)), "x", axis=0, tiled=True
    )

    chunk = value_cols // layers
    last = contract(grad, out_full[layers - 1], 1, 0).astype(BF)
    inputs, scaled, projected, inverse, last_sum = [], [], [], [], []
    for layer in range(layers):
        widened = state.astype(F32)
        squares = jnp.sum(widened * widened, axis=-1, keepdims=True)
        scaled_input = (widened * gains[layer][None, :]).astype(BF)
        high, low_part = split_pair(squares)
        total = gathered_sum(
            jnp.concatenate(
                [
                    contract(scaled_input, value_full[layer], 1, 0).astype(BF),
                    last[:, layer * chunk : (layer + 1) * chunk],
                    contract(scaled_input, downs_full[layer], 1, 1).astype(BF),
                    high,
                    low_part,
                ],
                axis=1,
            )
        )
        side = value_cols + chunk
        mean = (total[:, side + packed : side + packed + 1] + total[:, side + packed + 1 :]) / width
        inv = lax.rsqrt(mean + EPSILON)
        value_part, low_piece = total[:, :value_cols], total[:, side : side + packed]
        inputs.append(state)
        scaled.append(scaled_input)
        projected.append((value_part, low_piece))
        inverse.append(inv)
        last_sum.append(total[:, value_cols:side])
        if layer + 1 < layers:
            low = (low_piece * inv * coef).astype(BF)
            value = (value_part * inv + contract(low, ups[layer], 1, 0)).astype(BF)
            state = (widened + contract(value, out_full[layer], 1, 1)).astype(BF)

    blocks = [None] * layers
    extra = -(-packed // rows)
    for layer in reversed(range(layers)):
        if layer + 1 < layers:
            value_sum = gathered_sum(contract(grad, out_full[layer], 1, 0).astype(BF))
        else:
            value_sum = jnp.concatenate(last_sum, axis=1)
        value_grad = value_sum.astype(BF)
        low_grad = (contract(value_grad, ups[layer], 1, 1) * coef).astype(BF)
        inv = inverse[layer]
        value_part, low_piece = projected[layer]
        wide_value, wide_low = value_grad.astype(F32), low_grad.astype(F32)
        mixed_value, mixed_low = (wide_value * inv).astype(BF), (wide_low * inv).astype(BF)
        if layer > 0:
            inner = jnp.sum(value_part * wide_value, axis=1, keepdims=True)
            inner = inner + jnp.sum(low_piece * wide_low, axis=1, keepdims=True)
            kappa = inv * inv * inv * inner / width
            back = contract(mixed_value, value_full[layer], 1, 1)
            back = back + contract(mixed_low, downs_full[layer], 1, 0)
            grad = (
                grad.astype(F32)
                + gains[layer][None, :] * back
                - kappa * inputs[layer].astype(F32)
            ).astype(BF)
        down = contract(mixed_low, scaled[layer], 0, 0)
        down = down.reshape(packed, nz, nc, rows).transpose(2, 1, 0, 3)
        low = (low_piece * inv * coef).astype(BF)
        chosen = lax.dynamic_index_in_dim(
            value_grad.reshape(nx * tokens, nz, nx, -1), xi, 2, keepdims=False
        )
        each = chosen.shape[2] // nc
        up = contract(chosen.reshape(nx * tokens, -1), low, 0, 0)
        up = up.reshape(nz, nc, each, packed).transpose(1, 0, 2, 3)
        up = jnp.pad(up, ((0, 0), (0, 0), (0, 0), (0, extra * rows - packed)))
        block = jnp.concatenate(
            [down] + [up[..., k * rows : (k + 1) * rows] for k in range(extra)], axis=2
        ).astype(BF)
        blocks[layer] = summed(exchanged(block, "c")).astype(BF)

    total = summed(exchanged(jnp.stack(blocks), "y")).astype(BF)
    total = summed(exchanged(total, "z"))
    up = jnp.concatenate(
        [total[packed + k * each : packed + (k + 1) * each] for k in range(extra)], axis=1
    )[:, :packed]
    return (total[:packed].T[None], up.T[None])


def solution(mesh):
    shape = mesh.devices.shape
    cores, across = 2, 4
    split = Mesh(
        mesh.devices.reshape(shape[0], shape[1] // (across * cores), across, cores),
        ("y", "z", "x", "c"),
    )
    fsdp = ("z", "x", "c")
    placed = (
        P(None, fsdp, None),
        P(None, fsdp, None),
        P("y", fsdp, None),
        P("y", None, fsdp),
        P("y", None, None),
        P("y", None, None),
        P("y", None),
        P(None, fsdp),
        P(),
    )
    return jax.shard_map(
        local,
        mesh=split,
        in_specs=placed,
        out_specs=(P("y", fsdp, None), P("y", None, fsdp)),
        check_vma=False,
    )
```

profile of v0, /device:TPU:2, one launch (start us, length us, event | category | flops | bytes accessed | tf_op | source)
XLA Modules:
  0.0 391.7 jit_solution(12321162908527013947)
XLA Ops:
  14.2 5.7 %all-to-all-start = ((bf16[4,2,32,2048]{3,2,1,0:T(8,128)(2,1)}), bf16[4,2,32,2048]{3,2,1,0:T(8,128)(2,1)S(1)}, u32[]{:S(2)}, u32[]{:S(2)}) async-start(bf16[4,2,32,2048]{3,2,1,0:T(8,128)(2,1)} %reshape.261), calls=%async_computation | async-start | bytes 2097152 | tf_op jit(solution)/shard_map/all_to_all | solution.py:39
  23.8 5.5 %reshape.264 = bf16[160,8,4,256]{3,2,1,0:T(4,128)(2,1)} reshape(bf16[160,8192]{1,0:T(8,128)(2,1)} %bitcast.315) | data formatting | bytes 5242880 | tf_op jit(solution)/shard_map/reshape | solution.py:95
  29.3 5.6 %dynamic-slice_reduce_fusion = bf16[160,8,256]{2,1,0:T(8,128)(2,1)S(1)} fusion(bf16[160,8,4,256]{3,2,1,0:T(4,128)(2,1)} %reshape.264, s32[]{:T(128)S(6)} %select_n.36), kind=kLoop, calls=%fused_computation.52 | loop fusion | bytes 1310724 | tf_op jit(solution)/shard_map/jit(dynamic_index_in_dim)/dynamic_slice | solution.py:94
  36.0 13.0 %all_gather.63 = bf16[4,160,512]{2,1,0:T(8,128)(2,1)S(1)} all-gather(bf16[1,160,512]{2,1,0:T(8,128)(2,1)S(1)} %copy-done.30), channel_id=1, replica_groups=mesh['y'=4,'z'=8,'x'=4,'c'=2] {'y'}, dimensions={0}, use_global_device_ids=true | all-gather | bytes 819200 | tf_op jit(solution)/shard_map/all_gather | solution.py:103
  50.9 4.6 %all-to-all-start.1 = ((bf16[4,160,2048]{2,1,0:T(8,128)(2,1)}), bf16[4,160,2048]{2,1,0:T(8,128)(2,1)}, u32[]{:S(2)}, u32[]{:S(2)}) async-start(bf16[4,160,2048]{2,1,0:T(8,128)(2,1)} %broadcast_in_dim.35), calls=%async_computation.1 | async-start | bytes 5242880 | tf_op jit(solution)/shard_map/all_to_all | solution.py:39
  55.5 12.0 %all_gather.62 = f32[128,160]{1,0:T(8,128)S(1)} all-gather(f32[32,160]{1,0:T(8,128)S(1)} %broadcast_in_dim.65), channel_id=1, replica_groups=mesh['y'=4,'z'=8,'x'=4,'c'=2] {'x'}, dimensions={0}, use_global_device_ids=true | all-gather | bytes 102400 | tf_op jit(solution)/shard_map/all_gather | solution.py:106
  67.6 44.8 %all-gather.8 = f32[4,1,2048]{2,1,0:T(1,128)S(1)} all-gather(f32[1,1,2048]{2,1,0:T(1,128)S(1)} %bitcast.353), channel_id=1, replica_groups=mesh['y'=4,'z'=8,'x'=4,'c'=2] {'y'}, dimensions={0}, use_global_device_ids=true | all-gather | bytes 40960 | tf_op jit(solution)/shard_map/all_gather | solution.py:102
  117.5 17.1 %all-gather.11.cloned.1.call-done = bf16[8192,1024]{1,0:T(8,128)(2,1)} async-done(((bf16[128,1024]{1,0:T(8,128)(2,1)}), bf16[8192,1024]{1,0:T(8,128)(2,1)}) %all-gather.11.cloned.1.call-update) | async-done | bytes 16777232 | tf_op jit(solution)/shard_map/all_gather | solution.py:74
  139.6 14.7 %all-gather.1 = bf16[512,802]{1,0:T(8,128)(2,1)S(1)} all-gather(bf16[128,802]{1,0:T(8,128)(2,1)S(1)} %concatenate.52), channel_id=3, replica_groups=mesh['y'=4,'z'=8,'x'=4,'c'=2] {'x'}, dimensions={0}, use_global_device_ids=true | all-gather | bytes 1026560 | tf_op jit(solution)/shard_map/all_gather | solution.py:47
  154.8 3.3 multiply_reduce_fusion.2
  162.4 13.8 %all-gather.2 = bf16[512,802]{1,0:T(8,128)(2,1)S(1)} all-gather(bf16[128,802]{1,0:T(8,128)(2,1)S(1)} %concatenate.53), channel_id=4, replica_groups=mesh['y'=4,'z'=8,'x'=4,'c'=2] {'x'}, dimensions={0}, use_global_device_ids=true | all-gather | bytes 1026560 | tf_op jit(solution)/shard_map/all_gather | solution.py:47
  177.2 3.4 multiply_reduce_fusion.1
  184.8 14.2 %all-gather.3 = bf16[512,802]{1,0:T(8,128)(2,1)S(1)} all-gather(bf16[128,802]{1,0:T(8,128)(2,1)S(1)} %concatenate.54), channel_id=5, replica_groups=mesh['y'=4,'z'=8,'x'=4,'c'=2] {'x'}, dimensions={0}, use_global_device_ids=true | all-gather | bytes 1026560 | tf_op jit(solution)/shard_map/all_gather | solution.py:47
  205.6 3.5 multiply_reduce_fusion
  210.6 2.9 fusion.33
  216.7 13.6 %all-gather.4 = bf16[512,802]{1,0:T(8,128)(2,1)S(1)} all-gather(bf16[128,802]{1,0:T(8,128)(2,1)S(1)} %concatenate.55), channel_id=6, replica_groups=mesh['y'=4,'z'=8,'x'=4,'c'=2] {'x'}, dimensions={0}, use_global_device_ids=true | all-gather | bytes 1026560 | tf_op jit(solution)/shard_map/all_gather | solution.py:47
  238.8 2.5 fusion.27
  246.2 12.8 %all-gather.5 = bf16[512,512]{1,0:T(8,128)(2,1)S(1)} all-gather(bf16[128,512]{1,0:T(8,128)(2,1)S(1)} %fusion.34), channel_id=7, replica_groups=mesh['y'=4,'z'=8,'x'=4,'c'=2] {'x'}, dimensions={0}, use_global_device_ids=true | all-gather | bytes 655360 | tf_op jit(solution)/shard_map/all_gather | solution.py:47
  262.8 2.5 fusion.24
  268.1 2.2 fusion.36
  270.3 12.8 %all-gather.6 = bf16[512,512]{1,0:T(8,128)(2,1)S(1)} all-gather(bf16[128,512]{1,0:T(8,128)(2,1)S(1)} %fusion.36), channel_id=8, replica_groups=mesh['y'=4,'z'=8,'x'=4,'c'=2] {'x'}, dimensions={0}, use_global_device_ids=true | all-gather | bytes 655360 | tf_op jit(solution)/shard_map/all_gather | solution.py:47
  286.0 2.4 fusion.21
  288.7 2.3 reshape.274
  291.2 4.3 %all_to_all.40 = bf16[2,8,176,128]{3,1,2,0:T(8,128)(2,1)S(1)} all-to-all(bf16[2,8,176,128]{3,1,2,0:T(8,128)(2,1)S(1)} %pad_maximum_fusion.4), channel_id=1, replica_groups=mesh['y'=4,'z'=8,'x'=4,'c'=2] {'c'}, dimensions={0} | all-to-all | bytes 1441792 | tf_op jit(solution)/shard_map/all_to_all | solution.py:39
  298.3 2.3 reshape.271
  301.8 4.5 %all_to_all.41 = bf16[2,8,176,128]{3,1,2,0:T(8,128)(2,1)S(1)} all-to-all(bf16[2,8,176,128]{3,1,2,0:T(8,128)(2,1)S(1)} %pad_maximum_fusion.3), channel_id=1, replica_groups=mesh['y'=4,'z'=8,'x'=4,'c'=2] {'c'}, dimensions={0} | all-to-all | bytes 1441792 | tf_op jit(solution)/shard_map/all_to_all | solution.py:39
  314.1 4.3 %all_to_all.42 = bf16[2,8,176,128]{3,1,2,0:T(8,128)(2,1)S(1)} all-to-all(bf16[2,8,176,128]{3,1,2,0:T(8,128)(2,1)S(1)} %pad_maximum_fusion.2), channel_id=1, replica_groups=mesh['y'=4,'z'=8,'x'=4,'c'=2] {'c'}, dimensions={0} | all-to-all | bytes 1441792 | tf_op jit(solution)/shard_map/all_to_all | solution.py:39
  321.9 2.7 fusion.38
  324.6 12.8 %all-gather.7 = bf16[512,512]{1,0:T(8,128)(2,1)S(1)} all-gather(bf16[128,512]{1,0:T(8,128)(2,1)S(1)} %fusion.38), channel_id=9, replica_groups=mesh['y'=4,'z'=8,'x'=4,'c'=2] {'x'}, dimensions={0}, use_global_device_ids=true | all-gather | bytes 655360 | tf_op jit(solution)/shard_map/all_gather | solution.py:47
  338.6 4.4 %all_to_all.43 = bf16[2,8,176,128]{3,2,1,0:T(8,128)(2,1)S(1)} all-to-all(bf16[2,8,176,128]{3,2,1,0:T(8,128)(2,1)S(1)} %copy.412), channel_id=1, replica_groups=mesh['y'=4,'z'=8,'x'=4,'c'=2] {'c'}, dimensions={0} | all-to-all | bytes 1441792 | tf_op jit(solution)/shard_map/all_to_all | solution.py:39
  343.4 22.3 %all_to_all.44 = bf16[4,8,176,128]{3,2,1,0:T(8,128)(2,1)S(1)} all-to-all(bf16[4,8,176,128]{3,2,1,0:T(8,128)(2,1)S(1)} %pad_maximum_fusion), channel_id=1, replica_groups=mesh['y'=4,'z'=8,'x'=4,'c'=2] {'y'}, dimensions={0} | all-to-all | bytes 2883584 | tf_op jit(solution)/shard_map/all_to_all | solution.py:39
  366.0 17.5 %all_to_all.45 = bf16[8,176,128]{2,1,0:T(8,128)(2,1)S(1)} all-to-all(bf16[8,176,128]{2,1,0:T(8,128)(2,1)S(1)} %reduce_sum.294), channel_id=1, replica_groups=mesh['y'=4,'z'=8,'x'=4,'c'=2] {'z'}, dimensions={0} | all-to-all | bytes 720896 | tf_op jit(solution)/shard_map/all_to_all | solution.py:39
  (271 shorter events, 85.4 us)
Async XLA Ops:
  7.2 127.4 %all-gather.11.cloned.1.call-start = ((), (), s32[]{:S(2)}) async-start(), calls=%async_computation.8 | async-start | bytes 17039360 | tf_op jit(solution)/shard_map/all_gather | solution.py:74
  12.8 7.1 %copy-start.56 = (s32[2,2]{1,0:T(2,128)S(1)}, s32[2,2]{1,0:T(2,128)}, u32[]{:S(2)}) copy-start(s32[2,2]{1,0:T(2,128)} %param.16) | copy-start | bytes 52
  12.8 7.7 %copy-start.55 = (s32[4]{0:T(128)S(1)}, s32[4]{0:T(128)}, u32[]{:S(2)}) copy-start(s32[4]{0:T(128)} %param.17) | copy-start | bytes 52
  12.9 10.2 %copy-start.40 = (f32[1,8192]{1,0:T(1,128)S(1)}, f32[1,8192]{1,0:T(1,128)}, u32[]{:S(2)}) copy-start(f32[1,8192]{1,0:T(1,128)} %param.15) | copy-start | bytes 98308
  14.2 34.9 %all-to-all-start = ((bf16[4,2,32,2048]{3,2,1,0:T(8,128)(2,1)}), bf16[4,2,32,2048]{3,2,1,0:T(8,128)(2,1)S(1)}, u32[]{:S(2)}, u32[]{:S(2)}) async-start(bf16[4,2,32,2048]{3,2,1,0:T(8,128)(2,1)} %reshape.261), calls=%async_computation | async-start | bytes 2097152 | tf_op jit(solution)/shard_map/all_to_all | solution.py:39
  29.3 6.7 %copy-start.30 = (bf16[1,160,512]{2,1,0:T(8,128)(2,1)S(1)}, bf16[1,160,512]{2,1,0:T(8,128)(2,1)}, u32[]{:S(2)}) copy-start(bf16[1,160,512]{2,1,0:T(8,128)(2,1)} %param.14) | copy-start | bytes 491524
  49.0 128.2 %copy-start = (bf16[4,160,512]{2,1,0:T(8,128)(2,1)}, bf16[4,160,512]{2,1,0:T(8,128)(2,1)S(1)}, u32[]{:S(2)}) copy-start(bf16[4,160,512]{2,1,0:T(8,128)(2,1)S(1)} %all_gather.63) | copy-start | bytes 1966084
  50.9 64.7 %all-to-all-start.1 = ((bf16[4,160,2048]{2,1,0:T(8,128)(2,1)}), bf16[4,160,2048]{2,1,0:T(8,128)(2,1)}, u32[]{:S(2)}, u32[]{:S(2)}) async-start(bf16[4,160,2048]{2,1,0:T(8,128)(2,1)} %broadcast_in_dim.35), calls=%async_computation.1 | async-start | bytes 5242880 | tf_op jit(solution)/shard_map/all_to_all | solution.py:39
  113.0 41.9 %copy-start.35 = (f32[1,1,2048]{2,1,0:T(1,128)}, f32[1,1,2048]{2,1,0:T(1,128)S(1)}, u32[]{:S(2)}) copy-start(f32[1,1,2048]{2,1,0:T(1,128)S(1)} %get-tuple-element.35) | copy-start | bytes 24580
  113.0 64.2 %copy-start.36 = (f32[1,1,2048]{2,1,0:T(1,128)}, f32[1,1,2048]{2,1,0:T(1,128)S(1)}, u32[]{:S(2)}) copy-start(f32[1,1,2048]{2,1,0:T(1,128)S(1)} %get-tuple-element.37) | copy-start | bytes 24580
  115.6 21.2 %copy-start.5 = (bf16[4,1,32,2048]{3,2,1,0:T(8,128)(2,1)}, bf16[4,1,32,2048]{3,2,1,0:T(8,128)(2,1)S(1)}, u32[]{:S(2)}) copy-start(bf16[4,1,32,2048]{3,2,1,0:T(8,128)(2,1)S(1)} %get-tuple-element.10) | copy-start | bytes 1572868
  184.7 20.9 %copy-start.38 = (f32[1,1,2048]{2,1,0:T(1,128)S(1)}, f32[1,1,2048]{2,1,0:T(1,128)}, u32[]{:S(2)}) copy-start(f32[1,1,2048]{2,1,0:T(1,128)} %get-tuple-element.34) | copy-start | bytes 24580
  244.0 15.1 %copy-start.8 = (bf16[128,2048]{1,0:T(8,128)(2,1)}, bf16[128,2048]{1,0:T(8,128)(2,1)S(1)}, u32[]{:S(2)}) copy-start(bf16[128,2048]{1,0:T(8,128)(2,1)S(1)} %fusion.15) | copy-start | bytes 1572868
  244.0 16.2 %copy-start.1 = (bf16[4,160,512]{2,1,0:T(8,128)(2,1)S(1)}, bf16[4,160,512]{2,1,0:T(8,128)(2,1)}, u32[]{:S(2)}) copy-start(bf16[4,160,512]{2,1,0:T(8,128)(2,1)} %copy-done) | copy-start | bytes 1966084
  244.0 18.8 %copy-start.44 = (f32[128]{0:T(128)S(1)}, f32[128]{0:T(128)}, u32[]{:S(2)}) copy-start(f32[128]{0:T(128)} %copy-done.43) | copy-start | bytes 1540
  260.2 5.1 %copy-start.13 = (bf16[128,2048]{1,0:T(8,128)(2,1)S(1)}, bf16[128,2048]{1,0:T(8,128)(2,1)}, u32[]{:S(2)}) copy-start(bf16[128,2048]{1,0:T(8,128)(2,1)} %get-tuple-element.5) | copy-start | bytes 1572868
  268.0 15.1 %copy-start.7 = (bf16[128,2048]{1,0:T(8,128)(2,1)}, bf16[128,2048]{1,0:T(8,128)(2,1)S(1)}, u32[]{:S(2)}) copy-start(bf16[128,2048]{1,0:T(8,128)(2,1)S(1)} %fusion.16) | copy-start | bytes 1572868
  268.0 15.1 %copy-start.3 = (f32[128,802]{1,0:T(8,128)S(1)}, f32[128,802]{1,0:T(8,128)}, u32[]{:S(2)}) copy-start(f32[128,802]{1,0:T(8,128)} %copy-done.2) | copy-start | bytes 1231876
  268.0 15.8 %copy-start.20 = (f32[128,160]{0,1:T(8,128)S(1)}, f32[128,160]{0,1:T(8,128)}, u32[]{:S(2)}) copy-start(f32[128,160]{0,1:T(8,128)} %copy-done.19) | copy-start | bytes 245764
  268.1 18.0 %copy-start.42 = (f32[128]{0:T(128)S(1)}, f32[128]{0:T(128)}, u32[]{:S(2)}) copy-start(f32[128]{0:T(128)} %copy-done.41) | copy-start | bytes 1540
  283.9 4.5 %copy-start.29 = (f32[128,160]{0,1:T(8,128)S(1)}, f32[128,160]{0,1:T(8,128)}, u32[]{:S(2)}) copy-start(f32[128,160]{0,1:T(8,128)} %copy.460) | copy-start | bytes 245764
  283.9 4.5 %copy-start.31 = (bf16[128,128]{0,1:T(8,128)(2,1)S(1)}, bf16[128,128]{0,1:T(8,128)(2,1)}, u32[]{:S(2)}) copy-start(bf16[128,128]{0,1:T(8,128)(2,1)} %copy.426) | copy-start | bytes 98308
  283.9 4.5 %copy-start.32 = (bf16[128,128]{0,1:T(8,128)(2,1)S(1)}, bf16[128,128]{0,1:T(8,128)(2,1)}, u32[]{:S(2)}) copy-start(bf16[128,128]{0,1:T(8,128)(2,1)} %copy.427) | copy-start | bytes 98308
  283.9 4.5 %copy-start.33 = (bf16[128,128]{0,1:T(8,128)(2,1)S(1)}, bf16[128,128]{0,1:T(8,128)(2,1)}, u32[]{:S(2)}) copy-start(bf16[128,128]{0,1:T(8,128)(2,1)} %copy.428) | copy-start | bytes 98308
  283.9 4.5 %copy-start.34 = (bf16[128,128]{0,1:T(8,128)(2,1)S(1)}, bf16[128,128]{0,1:T(8,128)(2,1)}, u32[]{:S(2)}) copy-start(bf16[128,128]{0,1:T(8,128)(2,1)} %copy.429) | copy-start | bytes 98308
  283.9 4.5 %copy-start.46 = (f32[128]{0:T(128)S(1)}, f32[128]{0:T(128)}, u32[]{:S(2)}) copy-start(f32[128]{0:T(128)} %copy-done.45) | copy-start | bytes 1540
  321.9 15.7 %copy-start.10 = (bf16[2048,128]{1,0:T(8,128)(2,1)S(1)}, bf16[2048,128]{1,0:T(8,128)(2,1)}, u32[]{:S(2)}) copy-start(bf16[2048,128]{1,0:T(8,128)(2,1)} %copy.442) | copy-start | bytes 1572868
  321.9 15.7 %copy-start.48 = (f32[128]{0:T(128)S(1)}, f32[128]{0:T(128)}, u32[]{:S(2)}) copy-start(f32[128]{0:T(128)} %copy-done.47) | copy-start | bytes 1540
  324.6 13.6 %copy-start.24 = (bf16[128,160]{0,1:T(8,128)(2,1)S(1)}, bf16[128,160]{0,1:T(8,128)(2,1)}, u32[]{:S(2)}) copy-start(bf16[128,160]{0,1:T(8,128)(2,1)} %copy-done.23) | copy-start | bytes 122884
  338.5 4.8 %copy-start.16 = (bf16[8,176,128]{2,1,0:T(8,128)(2,1)S(1)}, bf16[8,176,128]{2,1,0:T(8,128)(2,1)}, u32[]{:S(2)}) copy-start(bf16[8,176,128]{2,1,0:T(8,128)(2,1)} %copy.471) | copy-start | bytes 1081348
  338.5 4.8 %copy-start.17 = (bf16[8,176,128]{2,1,0:T(8,128)(2,1)S(1)}, bf16[8,176,128]{2,1,0:T(8,128)(2,1)}, u32[]{:S(2)}) copy-start(bf16[8,176,128]{2,1,0:T(8,128)(2,1)} %copy.472) | copy-start | bytes 1081348
  338.5 4.8 %copy-start.18 = (bf16[8,176,128]{2,1,0:T(8,128)(2,1)S(1)}, bf16[8,176,128]{2,1,0:T(8,128)(2,1)}, u32[]{:S(2)}) copy-start(bf16[8,176,128]{2,1,0:T(8,128)(2,1)} %copy.473) | copy-start | bytes 1081348
  (28 other events, 82.5 us)
Sparse Core Ops, SparseCore 0:
  10.7 123.7 all-gather.10
where the time goes:
time: 394 us; the launch traced here: 392 us
  blocking collectives  222 us (56%)
  matrix products  56.4 us (14%)
  local copies, waits for them, and re-layouts  53.8 us (14%)
  waiting for transfers between devices  17.1 us (4%)
  other arithmetic  16.3 us (4%)
  between operations  16 us (4%)
  starting transfers between devices  10.3 us (3%)
    all_gather x7, blocking collectives, gathered_sum(): return summed(lax.all_gather(partial, 'x', axis=0, tiled=False))  94.5 us
    all_to_all x6, blocking collectives, exchanged(): return lax.all_to_all(value, axis, split_axis=0, concat_axis=0, tiled=True)  57.5 us
    dot_general x31, matrix products, contract(): lax.dot_general(left, right, (((left_dim,), (right_dim,)), ((), ())), pre...  56.4 us
    all_gather x1, blocking collectives, local(): gains = lax.all_gather(gains_local, 'y', axis=0, tiled=False)  44.8 us
    all_gather x1, waiting for transfers between devices, local(): full = lax.all_gather(joined, GROUP, axis=0, tiled=False)  17.1 us
    all_gather x1, blocking collectives, local(): ups = lax.all_gather(adapter_up_weight[0], 'y', axis=0, tiled=False)  13 us
    all_gather x1, blocking collectives, local(): lax.all_gather(jnp.broadcast_to(coef_row, (tokens, packed)), 'x', axis=0,...  12 us
    all_to_all x2, starting transfers between devices, exchanged(): return lax.all_to_all(value, axis, split_axis=0, concat_axis=0, tiled=True)  10.3 us
  transfers between devices with their start and end apart: 3, of which 1 were waited for; matrix products, arithmetic and copies ran while one was open for 7% of the time, Pallas kernels for 0%

commit v1 on v0

v1 whole, which is shorter than its diff:
```python
import functools

import jax
import jax.numpy as jnp
from jax import lax
from jax.experimental import pallas as pl
from jax.experimental.layout import Layout, with_layout_constraint
from jax.experimental.pallas import tpu as pltpu
from jax.sharding import Mesh, PartitionSpec as P

ADAPTERS = 4
EPSILON = 1e-06
ADAPTER_ALPHA = 32.0
BF = jnp.bfloat16
F32 = jnp.float32
GROUP = ("y", "z", "c")
LANES = 128
STEP = 512
INTERPRET = False


def contract(left, right, left_dim, right_dim):
    return lax.dot_general(
        left, right, (((left_dim,), (right_dim,)), ((), ())), preferred_element_type=F32
    )


def coefficient_row(adapter, adapter_rank_blocks, packed, columns):
    rank_sizes = 8 * adapter_rank_blocks
    adapters = jnp.arange(ADAPTERS, dtype=jnp.int32)
    ends = jnp.sum(
        jnp.where(adapters[None, :] <= adapters[:, None], rank_sizes[None, :], 0), axis=1
    )
    column = jnp.arange(columns, dtype=jnp.int32)
    owner = jnp.sum((column[:, None] >= ends[None, :]).astype(jnp.int32), axis=1)
    rank = jnp.sum(jnp.where(adapters == adapter, rank_sizes, 0)).astype(F32)
    held = (owner == adapter) & (column < packed)
    return jnp.where(held, ADAPTER_ALPHA / rank, 0.0)[None, :]


def exchanged(value, axis):
    return lax.all_to_all(value, axis, split_axis=0, concat_axis=0, tiled=True)


def summed(value):
    return value.astype(F32).sum(axis=0)


def gathered(partial):
    return lax.all_gather(partial, "x", axis=0, tiled=False)


def token_stats(gathered_ref, value_cols, chunk, packed, width):
    total = gathered_ref[...].astype(F32).sum(axis=0)
    side = total[:, value_cols + chunk :]
    mean = (side[:, packed : packed + 1] + side[:, packed + 1 : packed + 2]) / width
    return total[:, :value_cols], side, lax.rsqrt(mean + EPSILON)


def forward_kernel(*refs, first, sizes):
    value_cols, chunk, packed, width = sizes
    if first:
        grad, last_out, state, value_w, down_w, gain, sent, last_sum, scaled = refs[:9]
        acc, side_acc, square_acc, last_acc = refs[9:]
    else:
        before, coef, up, state, out_w, value_w, down_w, gain, last_piece = refs[:9]
        sent, new_state, scaled = refs[9:12]
        acc, side_acc, square_acc, values = refs[12:]
    step = pl.program_id(0)

    @pl.when(step == 0)
    def _():
        acc[...] = jnp.zeros_like(acc)
        side_acc[...] = jnp.zeros_like(side_acc)
        square_acc[...] = jnp.zeros_like(square_acc)
        if first:
            last_acc[...] = jnp.zeros_like(last_acc)
        else:
            value_part, side, inv = token_stats(before, value_cols, chunk, packed, width)
            low = (side * inv * coef[...]).astype(BF)
            values[...] = (value_part * inv + contract(low, up[0], 1, 0)).astype(BF)

    if first:
        wide = state[...].astype(F32)
        last_acc[...] += contract(grad[...], last_out[0], 1, 0)
    else:
        wide = state[...].astype(F32) + contract(values[...], out_w[0], 1, 1)
        new_state[...] = wide.astype(BF)
        wide = new_state[...].astype(F32)
    square_acc[...] += jnp.sum(wide * wide, axis=1, keepdims=True)
    scaled_input = (wide * gain[0]).astype(BF)
    scaled[...] = scaled_input
    acc[...] += contract(scaled_input, value_w[0], 1, 0)
    side_acc[...] += contract(scaled_input, down_w[0], 1, 1)

    @pl.when(step == pl.num_programs(0) - 1)
    def _():
        sent[:, :value_cols] = acc[...].astype(BF)
        if first:
            last = last_acc[...].astype(BF)
            last_sum[...] = last
            sent[:, value_cols : value_cols + chunk] = last[:, :chunk]
        else:
            sent[:, value_cols : value_cols + chunk] = last_piece[...]
        squares = square_acc[:, :1]
        high = squares.astype(BF).astype(F32)
        lane = lax.broadcasted_iota(jnp.int32, side_acc.shape, 1)
        side = jnp.where(lane == packed, high, side_acc[...])
        side = jnp.where(lane == packed + 1, squares - high, side)
        sent[:, value_cols + chunk :] = side.astype(BF)


def backward_kernel(*refs, last, bottom, sizes, spots):
    value_cols, chunk, packed, width = sizes
    nz, nx, nc, each = spots
    refs = list(refs)
    take = lambda n: [refs.pop(0) for _ in range(n)]
    where, = take(1)
    pieces = take(value_cols // chunk if last else 1)
    before, coef, up, scaled = take(4)
    if not bottom:
        state, grad, value_w, down_w, gain, out_w = take(6)
    own, other = take(2)
    if not bottom:
        sent, new_grad = take(2)
    mixed_low, raised = take(2)
    if not bottom:
        mixed_value, kappa, acc = take(3)
    step = pl.program_id(0)
    xi, ci = where[0], where[1]

    @pl.when(step == 0)
    def _():
        summed_pieces = [piece[...].astype(F32).sum(axis=0) for piece in pieces]
        total = summed_pieces[0] if len(pieces) == 1 else jnp.concatenate(summed_pieces, axis=1)
        value_grad = total.astype(BF)
        wide_value = value_grad.astype(F32)
        low_grad = (contract(value_grad, up[0], 1, 1) * coef[...]).astype(BF)
        wide_low = low_grad.astype(F32)
        value_part, side, inv = token_stats(before, value_cols, chunk, packed, width)
        mixed_low[...] = (wide_low * inv).astype(BF)
        if not bottom:
            mixed_value[...] = (wide_value * inv).astype(BF)
            inner = jnp.sum(value_part * wide_value, axis=1, keepdims=True)
            inner = inner + jnp.sum(side * wide_low, axis=1, keepdims=True)
            kappa[...] = jnp.broadcast_to(inv * inv * inv * inner / width, kappa.shape)
            acc[...] = jnp.zeros_like(acc)
        low = (side * inv * coef[...]).astype(BF)
        raised[...] = contract(value_grad, low, 0, 0)
        for z in range(nz):
            for target, core in ((own, ci), (other, 1 - ci)):
                row = pl.multiple_of((z * nx + xi) * nc * each + core * each, each)
                piece = raised[pl.ds(row, each), :]
                target[z, packed:, :] = jnp.concatenate(
                    [piece[:, k * LANES : (k + 1) * LANES] for k in range(piece.shape[1] // LANES)],
                    axis=0,
                ).astype(BF)

    lowered = contract(mixed_low[...], scaled[...], 0, 0)[:packed]
    per_step = scaled.shape[1] // (nc * LANES)
    for k in range(per_step):
        start = k * nc * LANES
        one = lowered[:, start : start + LANES]
        two = lowered[:, start + LANES : start + 2 * LANES]
        own[step * per_step + k, :packed, :] = jnp.where(ci == 0, one, two).astype(BF)
        other[step * per_step + k, :packed, :] = jnp.where(ci == 0, two, one).astype(BF)
    if not bottom:
        back = contract(mixed_value[...], value_w[0], 1, 1)
        back = back + contract(mixed_low[...], down_w[0], 1, 0)
        wide = grad[...].astype(F32) + gain[0] * back - kappa[:, :1] * state[...].astype(F32)
        updated = wide.astype(BF)
        new_grad[...] = updated
        acc[...] += contract(updated, out_w[0], 1, 0)

        @pl.when(step == pl.num_programs(0) - 1)
        def _():
            sent[...] = acc[...].astype(BF)


def whole(shape):
    return pl.BlockSpec(shape, lambda i: (0,) * len(shape))


def columns(tokens):
    return pl.BlockSpec((tokens, STEP), lambda i: (0, i))


def weight(layer, half, cols):
    return pl.BlockSpec((1, STEP, cols), lambda i: (layer, i, half))


def layered(layer, shape):
    return pl.BlockSpec((1,) + shape, lambda i: (layer,) + (0,) * len(shape))


def along(layer, rows):
    return pl.BlockSpec((1, rows, STEP), lambda i: (layer, 0, i))


def local(
    residual_input,
    output_gradient,
    value_projection_weight,
    output_weight,
    adapter_down_weight,
    adapter_up_weight,
    input_norm_scale,
    segment_adapter_index,
    adapter_rank_blocks,
):
    ny, nz, nx, nc = (lax.axis_size(name) for name in ("y", "z", "x", "c"))
    yi, zi, xi, ci = (lax.axis_index(name) for name in ("y", "z", "x", "c"))
    rows = value_projection_weight.shape[1]
    value_cols = value_projection_weight.shape[2]
    packed = adapter_down_weight.shape[2]
    width = adapter_down_weight.shape[1]
    both = value_cols + packed
    layers = ny
    lanes = nc * rows
    depth = nz * lanes

    joined = jnp.concatenate([value_projection_weight[0], output_weight[0].T], axis=1)
    joined = with_layout_constraint(joined, Layout(major_to_minor=(0, 1)))
    full = lax.all_gather(joined, GROUP, axis=0, tiled=False)
    full = with_layout_constraint(full, Layout(major_to_minor=(0, 1, 2)))
    full = full.reshape(layers, depth, 2 * value_cols)

    all_tokens = residual_input.shape[0] * residual_input.shape[1]
    tokens = all_tokens // ny
    first = yi * tokens
    own = jnp.stack(
        [
            lax.dynamic_slice(array.reshape(all_tokens, width), (first, 0), (tokens, width))
            for array in (residual_input, output_gradient)
        ]
    )
    own = own.reshape(2, tokens, nz, nx, lanes).transpose(3, 0, 1, 2, 4)
    spread = exchanged(own.reshape(nx, 2, tokens, depth), "x")
    state = spread[:, 0].reshape(nx * tokens, depth)
    grad = spread[:, 1].reshape(nx * tokens, depth)

    down_local = lax.dynamic_index_in_dim(
        adapter_down_weight[0].T.reshape(packed, nz, nx, lanes), xi, 2, keepdims=False
    ).reshape(1, packed, depth)
    downs_full = exchanged(jnp.broadcast_to(down_local, (layers, packed, depth)), "y")
    padded = -(-packed // LANES) * LANES
    downs_full = jnp.pad(downs_full, ((0, 0), (0, padded - packed), (0, 0)))

    gains_local = lax.dynamic_index_in_dim(
        input_norm_scale.reshape(nz, nx, lanes), xi, 1, keepdims=False
    ).reshape(depth)
    gains = lax.all_gather(gains_local, "y", axis=0, tiled=False)
    gains = gains.reshape(layers, 1, depth)
    ups = lax.all_gather(adapter_up_weight[0], "y", axis=0, tiled=False)
    ups = jnp.pad(ups, ((0, 0), (0, padded - packed), (0, 0)))
    adapter = lax.dynamic_index_in_dim(segment_adapter_index.reshape(ny), yi, 0, keepdims=False)
    coef_row = coefficient_row(adapter, adapter_rank_blocks, packed, padded)
    coef = lax.all_gather(
        jnp.broadcast_to(coef_row, (tokens, padded)), "x", axis=0, tiled=True
    )

    count = nx * tokens
    chunk = value_cols // layers
    sizes = (value_cols, chunk, packed, width)
    wire = value_cols + chunk + padded
    each = value_cols // (nz * nx * nc)
    steps = depth // STEP
    shape = jax.ShapeDtypeStruct
    call = functools.partial(pl.pallas_call, grid=(steps,), interpret=INTERPRET)
    sent_shape, wide_shape = shape((count, wire), BF), shape((count, depth), BF)
    sums = [
        pltpu.VMEM((count, value_cols), F32),
        pltpu.VMEM((count, padded), F32),
        pltpu.VMEM((count, LANES), F32),
    ]
    top = layers - 1

    sent, last, scaled_input = call(
        functools.partial(forward_kernel, first=True, sizes=sizes),
        out_shape=(sent_shape, shape((count, value_cols), BF), wide_shape),
        in_specs=[
            columns(count),
            weight(top, 1, value_cols),
            columns(count),
            weight(0, 0, value_cols),
            along(0, padded),
            along(0, 1),
        ],
        out_specs=(whole((count, wire)), whole((count, value_cols)), columns(count)),
        scratch_shapes=sums + [pltpu.VMEM((count, value_cols), F32)],
    )(grad, full, state, full, downs_full, gains)
    arrived, inputs, scaled = [gathered(sent)], [state], [scaled_input]
    for layer in range(1, layers):
        sent, state, scaled_input = call(
            functools.partial(forward_kernel, first=False, sizes=sizes),
            out_shape=(sent_shape, wide_shape, wide_shape),
            in_specs=[
                whole((nx, count, wire)),
                whole((count, padded)),
                layered(layer - 1, (padded, value_cols)),
                columns(count),
                weight(layer - 1, 1, value_cols),
                weight(layer, 0, value_cols),
                along(layer, padded),
                along(layer, 1),
                pl.BlockSpec((count, chunk), lambda i, layer=layer: (0, layer)),
            ],
            out_specs=(whole((count, wire)), columns(count), columns(count)),
            scratch_shapes=sums + [pltpu.VMEM((count, value_cols), BF)],
        )(arrived[-1], coef, ups, state, full, full, downs_full, gains, last)
        arrived.append(gathered(sent))
        inputs.append(state)
        scaled.append(scaled_input)

    spots = (nz, nx, nc, each)
    place_ids = jnp.stack([xi, ci]).astype(jnp.int32)
    block_rows = packed + each * (padded // LANES)
    block_shape = (nz, block_rows, LANES)
    kept, crossed = [None] * layers, [None] * layers
    pieces, piece_specs = arrived, [
        pl.BlockSpec((nx, count, chunk), lambda i: (0, 0, value_cols // chunk))
    ] * layers
    for layer in reversed(range(layers)):
        bottom = layer == 0
        operands = [place_ids, *pieces, arrived[layer], coef, ups, scaled[layer]]
        specs = [
            pl.BlockSpec(memory_space=pltpu.SMEM),
            *piece_specs,
            whole((nx, count, wire)),
            whole((count, padded)),
            layered(layer, (padded, value_cols)),
            columns(count),
        ]
        outs = [shape(block_shape, BF)] * 2
        out_specs = [whole(block_shape)] * 2
        scratch = [pltpu.VMEM((count, padded), BF), pltpu.VMEM((value_cols, padded), F32)]
        if not bottom:
            operands += [inputs[layer], grad, full, downs_full, gains, full]
            specs += [
                columns(count),
                columns(count),
                weight(layer, 0, value_cols),
                along(layer, padded),
                along(layer, 1),
                weight(layer - 1, 1, value_cols),
            ]
            outs += [shape((count, value_cols), BF), wide_shape]
            out_specs += [whole((count, value_cols)), columns(count)]
            scratch += [
                pltpu.VMEM((count, value_cols), BF),
                pltpu.VMEM((count, LANES), F32),
                pltpu.VMEM((count, value_cols), F32),
            ]
        results = call(
            functools.partial(
                backward_kernel, last=layer == top, bottom=bottom, sizes=sizes, spots=spots
            ),
            out_shape=outs,
            in_specs=specs,
            out_specs=out_specs,
            scratch_shapes=scratch,
        )(*operands)
        kept[layer] = results[0]
        crossed[layer] = lax.ppermute(results[1], "c", [(j, 1 - j) for j in range(nc)])
        if not bottom:
            grad = results[3]
            pieces = [gathered(results[2])]
            piece_specs = [whole((nx, count, value_cols))]

    total = (jnp.stack(kept).astype(F32) + jnp.stack(crossed).astype(F32)).astype(BF)
    total = summed(exchanged(total, "y")).astype(BF)
    total = summed(exchanged(total, "z"))
    up = jnp.concatenate(
        [total[packed + k * each : packed + (k + 1) * each] for k in range(padded // LANES)],
        axis=1,
    )[:, :packed]
    return (total[:packed].T[None], up.T[None])


def solution(mesh):
    shape = mesh.devices.shape
    cores, across = 2, 4
    split = Mesh(
        mesh.devices.reshape(shape[0], shape[1] // (across * cores), across, cores),
        ("y", "z", "x", "c"),
    )
    fsdp = ("z", "x", "c")
    placed = (
        P(None, fsdp, None),
        P(None, fsdp, None),
        P("y", fsdp, None),
        P("y", None, fsdp),
        P("y", None, None),
        P("y", None, None),
        P("y", None),
        P(None, fsdp),
        P(),
    )
    return jax.shard_map(
        local,
        mesh=split,
        in_specs=placed,
        out_specs=(P("y", fsdp, None), P("y", None, fsdp)),
        check_vma=False,
    )
```

time: 394 us -> 334 us (0.85)
  matrix products: 56.4 us -> 0 us
  Pallas kernels: 0 us -> 52.1 us
  local copies, waits for them, and re-layouts: 53.8 us -> 22.4 us
  blocking collectives: 222 us -> 214 us
  other arithmetic: 16.3 us -> 8.31 us
  waiting for transfers between devices: 17.1 us -> 10.2 us
    dot_general x31 -> x0, matrix products: 56.4 us -> none  [contract(): lax.dot_general(left, right, (((left_dim,), (right_dim,)), ((), ())), pre...]
    pallas_call x0 -> x8, Pallas kernels: none -> 52.1 us  [the longest x4 26.4 us: local(): call(functools.partial(backward_kernel, last=layer == top, bottom=bottom,...]
    all_gather x1, blocking collectives: 44.8 us -> 13 us  [local(): gains = lax.all_gather(gains_local, 'y', axis=0, tiled=False)]
    all_gather x1, blocking collectives: 13 us -> 44.2 us  [local(): ups = lax.all_gather(adapter_up_weight[0], 'y', axis=0, tiled=False)]
    all_to_all x6 -> x2, blocking collectives: 57.5 us -> 41.4 us  [exchanged(): return lax.all_to_all(value, axis, split_axis=0, concat_axis=0, tiled=True)]
    all_gather x1, waiting for transfers between devices: 17.1 us -> 4.48 us  [local(): full = lax.all_gather(joined, GROUP, axis=0, tiled=False)]
    all_gather x8, blocking collectives: 107 us -> 115 us  [the longest x7 103 us: gathered(): return lax.all_gather(partial, 'x', axis=0, tiled=False)]
    reshape x6 -> x0, local copies, waits for them, and re-layouts: 7.28 us -> none  [local(): down = down.reshape(packed, nz, nc, rows).transpose(2, 1, 0, 3)]
  transfers between devices with their start and end apart: 3 -> 7, of which waited for: 1 -> 3; matrix products, arithmetic and copies ran while one was open for 7% -> 7% of each run, Pallas kernels for 0% -> 6%
where the time goes in v1:
time: 334 us; the launch traced here: 333 us
  blocking collectives  214 us (64%)
  Pallas kernels  52.1 us (16%)
  local copies, waits for them, and re-layouts  22.4 us (7%)
  between operations  15 us (4%)
  starting transfers between devices  11.5 us (3%)
  waiting for transfers between devices  10.2 us (3%)
  other arithmetic  8.31 us (2%)
    all_gather x7, blocking collectives, gathered(): return lax.all_gather(partial, 'x', axis=0, tiled=False)  103 us
    all_gather x1, blocking collectives, local(): ups = lax.all_gather(adapter_up_weight[0], 'y', axis=0, tiled=False)  44.2 us
    all_to_all x2, blocking collectives, exchanged(): return lax.all_to_all(value, axis, split_axis=0, concat_axis=0, tiled=True)  41.4 us
    pallas_call x4, Pallas kernels, local(): call(functools.partial(backward_kernel, last=layer == top, bottom=bottom,...  26.4 us
    pallas_call x3, Pallas kernels, local(): call(functools.partial(forward_kernel, first=False, sizes=sizes), out_sha...  20.4 us
    all_gather x1, blocking collectives, local(): gains = lax.all_gather(gains_local, 'y', axis=0, tiled=False)  13 us
    all_gather x1, blocking collectives, local(): lax.all_gather(jnp.broadcast_to(coef_row, (tokens, padded)), 'x', axis=0,...  11.8 us
    all_to_all x2, starting transfers between devices, exchanged(): return lax.all_to_all(value, axis, split_axis=0, concat_axis=0, tiled=True)  11.2 us
  transfers between devices with their start and end apart: 7, of which 3 were waited for; matrix products, arithmetic and copies ran while one was open for 7% of the time, Pallas kernels for 6%

profile of v1, /device:TPU:2, one launch (start us, length us, event | category | flops | bytes accessed | tf_op | source)
XLA Modules:
  0.0 333.2 jit_solution(16066641623774261802)
XLA Ops:
  8.2 1.7 pad_maximum_fusion
  14.1 6.4 %all-to-all-start = ((bf16[4,2,32,2048]{3,2,1,0:T(8,128)(2,1)}), bf16[4,2,32,2048]{3,2,1,0:T(8,128)(2,1)}, u32[]{:S(2)}, u32[]{:S(2)}) async-start(bf16[4,2,32,2048]{3,2,1,0:T(8,128)(2,1)} %reshape.50), calls=%async_computation | async-start | bytes 2097152 | tf_op jit(solution)/shard_map/all_to_all | solution.py:42
  20.6 4.3 %reshape.52 = bf16[160,8,4,256]{3,2,1,0:T(4,128)(2,1)S(1)} reshape(bf16[160,8192]{1,0:T(8,128)(2,1)} %bitcast.76) | data formatting | bytes 5242880 | tf_op jit(solution)/shard_map/reshape | solution.py:243
  24.9 3.8 %dynamic-slice_reduce_fusion = bf16[160,8,256]{2,1,0:T(8,128)(2,1)S(1)} fusion(bf16[160,8,4,256]{3,2,1,0:T(4,128)(2,1)S(1)} %reshape.52, s32[]{:T(128)S(6)} %select_n.31), kind=kLoop, calls=%fused_computation.1 | loop fusion | bytes 1310724 | tf_op jit(solution)/shard_map/jit(dynamic_index_in_dim)/dynamic_slice | solution.py:242
  28.9 3.8 %all-to-all-done = bf16[4,2,32,2048]{3,2,1,0:T(8,128)(2,1)} async-done(((bf16[4,2,32,2048]{3,2,1,0:T(8,128)(2,1)}), bf16[4,2,32,2048]{3,2,1,0:T(8,128)(2,1)}, u32[]{:S(2)}, u32[]{:S(2)}) %all-to-all-start) | async-done | bytes 1048608 | tf_op jit(solution)/shard_map/all_to_all | solution.py:42
  32.7 1.8 broadcast_in_dim.49
  34.6 4.8 %all-to-all-start.1 = ((bf16[4,160,2048]{2,1,0:T(8,128)(2,1)}), bf16[4,160,2048]{2,1,0:T(8,128)(2,1)S(1)}, u32[]{:S(2)}, u32[]{:S(2)}) async-start(bf16[4,160,2048]{2,1,0:T(8,128)(2,1)} %broadcast_in_dim.49), calls=%async_computation.1 | async-start | bytes 5242880 | tf_op jit(solution)/shard_map/all_to_all | solution.py:42
  43.5 44.2 %all_gather.63 = bf16[4,160,512]{2,1,0:T(8,128)(2,1)S(1)} all-gather(bf16[1,160,512]{2,1,0:T(8,128)(2,1)S(1)} %copy-done.3), channel_id=1, replica_groups=mesh['y'=4,'z'=8,'x'=4,'c'=2] {'y'}, dimensions={0}, use_global_device_ids=true | all-gather | bytes 819200 | tf_op jit(solution)/shard_map/all_gather | solution.py:254
  88.7 13.0 %all-gather.8.refs_5_.refs_7_.refs_13_.refs_10_ = f32[4,1,2048]{2,1,0:T(1,128)} all-gather(f32[1,1,2048]{2,1,0:T(1,128)S(1)} %bitcast.94), channel_id=1, replica_groups=mesh['y'=4,'z'=8,'x'=4,'c'=2] {'y'}, dimensions={0}, use_global_device_ids=true | all-gather | bytes 40960 | tf_op jit(solution)/shard_map/all_gather | solution.py:252
  102.5 11.8 %all_gather.62.refs_1_.refs_6_.refs_3_ = f32[128,256]{1,0:T(8,128)} all-gather(f32[32,256]{1,0:T(8,128)S(1)} %broadcast_in_dim.55), channel_id=1, replica_groups=mesh['y'=4,'z'=8,'x'=4,'c'=2] {'x'}, dimensions={0}, use_global_device_ids=true | all-gather | bytes 163840 | tf_op jit(solution)/shard_map/all_gather | solution.py:258
  114.9 2.4 fusion.2
  117.3 2.4 pad.8.refs_4_.refs_6_.refs_12_.refs_9_
  119.7 4.5 %all-gather.11.cloned.1.call-done = bf16[8192,1024]{1,0:T(8,128)(2,1)} async-done(((bf16[128,1024]{1,0:T(8,128)(2,1)}), bf16[8192,1024]{1,0:T(8,128)(2,1)}) %all-gather.11.cloned.1.call-update) | async-done | bytes 16777232 | tf_op jit(solution)/shard_map/all_gather | solution.py:224
  124.2 5.2 %shard_map.104 = (bf16[128,896]{1,0:T(8,128)(2,1)}, bf16[128,512]{1,0:T(8,128)(2,1)}, bf16[128,2048]{1,0:T(8,128)(2,1)}) custom-call(bf16[128,2048]{1,0:T(8,128)(2,1)} %bitcast.74, bf16[4,2048,1024]{2,1,0:T(8,128)(2,1)} %bitcast.47, bf16[128,2048]{1,0:T(8,128)(2,1)} %bitcast.72, bf16[4,2048,1024]{2,1,0:T(8,128)(2,1)} %bitcast.48, ...), custom_call_target="tpu_custom_call" | custom-call | tf_op jit(solution)/shard_map/pallas_call | solution.py:278
  129.4 15.8 %all-gather.1 = bf16[512,896]{1,0:T(8,128)(2,1)} all-gather(bf16[128,896]{1,0:T(8,128)(2,1)} %get-tuple-element.27), channel_id=3, replica_groups=mesh['y'=4,'z'=8,'x'=4,'c'=2] {'x'}, dimensions={0}, use_global_device_ids=true | all-gather | bytes 1146880 | tf_op jit(solution)/shard_map/all_gather | solution.py:50
  145.2 6.7 %shard_map.105 = (bf16[128,896]{1,0:T(8,128)(2,1)}, bf16[128,2048]{1,0:T(8,128)(2,1)}, bf16[128,2048]{1,0:T(8,128)(2,1)}) custom-call(bf16[4,128,896]{2,1,0:T(8,128)(2,1)} %bitcast.61, f32[128,256]{1,0:T(8,128)} %all_gather.62.refs_1_.refs_6_.refs_3_, bf16[4,256,512]{2,1,0:T(8,128)(2,1)} %pad.9.refs_2_.refs_7_.refs_4_, bf16[128,2048]{1,0:T(8,128)(2,1)} %bitcast.73, ...), custom_call_target="tpu_custom_call" | custom-call | tf_op jit(solution)/shard_map/pallas_call | solution.py:294
  151.9 15.7 %all-gather.2 = bf16[512,896]{1,0:T(8,128)(2,1)} all-gather(bf16[128,896]{1,0:T(8,128)(2,1)} %get-tuple-element.29), channel_id=4, replica_groups=mesh['y'=4,'z'=8,'x'=4,'c'=2] {'x'}, dimensions={0}, use_global_device_ids=true | all-gather | bytes 1146880 | tf_op jit(solution)/shard_map/all_gather | solution.py:50
  167.6 6.9 %shard_map.106 = (bf16[128,896]{1,0:T(8,128)(2,1)}, bf16[128,2048]{1,0:T(8,128)(2,1)}, bf16[128,2048]{1,0:T(8,128)(2,1)}) custom-call(bf16[4,128,896]{2,1,0:T(8,128)(2,1)} %bitcast.64, f32[128,256]{1,0:T(8,128)} %all_gather.62.refs_1_.refs_6_.refs_3_, bf16[4,256,512]{2,1,0:T(8,128)(2,1)} %pad.9.refs_2_.refs_7_.refs_4_, ...), custom_call_target="tpu_custom_call" | custom-call | tf_op jit(solution)/shard_map/pallas_call | solution.py:294
  174.6 14.6 %all-gather.3 = bf16[512,896]{1,0:T(8,128)(2,1)} all-gather(bf16[128,896]{1,0:T(8,128)(2,1)} %get-tuple-element.31), channel_id=5, replica_groups=mesh['y'=4,'z'=8,'x'=4,'c'=2] {'x'}, dimensions={0}, use_global_device_ids=true | all-gather | bytes 1146880 | tf_op jit(solution)/shard_map/all_gather | solution.py:50
  189.2 6.8 %shard_map.107 = (bf16[128,896]{1,0:T(8,128)(2,1)}, bf16[128,2048]{1,0:T(8,128)(2,1)}, bf16[128,2048]{1,0:T(8,128)(2,1)}) custom-call(bf16[4,128,896]{2,1,0:T(8,128)(2,1)} %bitcast.67, f32[128,256]{1,0:T(8,128)} %all_gather.62.refs_1_.refs_6_.refs_3_, bf16[4,256,512]{2,1,0:T(8,128)(2,1)} %pad.9.refs_2_.refs_7_.refs_4_, ...), custom_call_target="tpu_custom_call" | custom-call | tf_op jit(solution)/shard_map/pallas_call | solution.py:294
  195.9 14.8 %all-gather.4 = bf16[512,896]{1,0:T(8,128)(2,1)} all-gather(bf16[128,896]{1,0:T(8,128)(2,1)} %get-tuple-element.33), channel_id=6, replica_groups=mesh['y'=4,'z'=8,'x'=4,'c'=2] {'x'}, dimensions={0}, use_global_device_ids=true | all-gather | bytes 1146880 | tf_op jit(solution)/shard_map/all_gather | solution.py:50
  210.7 7.3 %shard_map.108 = (bf16[8,176,128]{2,1,0:T(8,128)(2,1)}, bf16[8,176,128]{2,1,0:T(8,128)(2,1)}, bf16[128,512]{1,0:T(8,128)(2,1)}, bf16[128,2048]{1,0:T(8,128)(2,1)}) custom-call(s32[2]{0:T(128)} %pad_add_fusion.refs_0_, bf16[4,128,896]{2,1,0:T(8,128)(2,1)} %bitcast.62, bf16[4,128,896]{2,1,0:T(8,128)(2,1)} %bitcast.65, bf16[4,128,896]{2,1,0:T(8,128)(2,1)} %bitcast.68, ...), custom_call_target="tpu_custom_call" | custom-call | tf_op jit(solution)/shard_map/pallas_call | solution.py:354
  218.1 14.2 %all-gather.5 = bf16[512,512]{1,0:T(8,128)(2,1)} all-gather(bf16[128,512]{1,0:T(8,128)(2,1)} %get-tuple-element.36), channel_id=7, replica_groups=mesh['y'=4,'z'=8,'x'=4,'c'=2] {'x'}, dimensions={0}, use_global_device_ids=true | all-gather | bytes 655360 | tf_op jit(solution)/shard_map/all_gather | solution.py:50
  232.3 7.2 %shard_map.109 = (bf16[8,176,128]{2,1,0:T(8,128)(2,1)}, bf16[8,176,128]{2,1,0:T(8,128)(2,1)}, bf16[128,512]{1,0:T(8,128)(2,1)}, bf16[128,2048]{1,0:T(8,128)(2,1)}) custom-call(s32[2]{0:T(128)} %pad_add_fusion.refs_0_, bf16[4,128,512]{2,1,0:T(8,128)(2,1)} %bitcast.80, bf16[4,128,896]{2,1,0:T(8,128)(2,1)} %bitcast.69, ...), custom_call_target="tpu_custom_call" | custom-call | tf_op jit(solution)/shard_map/pallas_call | solution.py:354
  239.6 14.2 %all-gather.6 = bf16[512,512]{1,0:T(8,128)(2,1)} all-gather(bf16[128,512]{1,0:T(8,128)(2,1)} %get-tuple-element.39), channel_id=8, replica_groups=mesh['y'=4,'z'=8,'x'=4,'c'=2] {'x'}, dimensions={0}, use_global_device_ids=true | all-gather | bytes 655360 | tf_op jit(solution)/shard_map/all_gather | solution.py:50
  253.8 7.3 %shard_map.110 = (bf16[8,176,128]{2,1,0:T(8,128)(2,1)}, bf16[8,176,128]{2,1,0:T(8,128)(2,1)}, bf16[128,512]{1,0:T(8,128)(2,1)}, bf16[128,2048]{1,0:T(8,128)(2,1)}) custom-call(s32[2]{0:T(128)} %pad_add_fusion.refs_0_, bf16[4,128,512]{2,1,0:T(8,128)(2,1)} %bitcast.79, bf16[4,128,896]{2,1,0:T(8,128)(2,1)} %bitcast.66, ...), custom_call_target="tpu_custom_call" | custom-call | tf_op jit(solution)/shard_map/pallas_call | solution.py:354
  261.2 14.2 %all-gather.7 = bf16[512,512]{1,0:T(8,128)(2,1)} all-gather(bf16[128,512]{1,0:T(8,128)(2,1)} %get-tuple-element.42), channel_id=9, replica_groups=mesh['y'=4,'z'=8,'x'=4,'c'=2] {'x'}, dimensions={0}, use_global_device_ids=true | all-gather | bytes 655360 | tf_op jit(solution)/shard_map/all_gather | solution.py:50
  275.4 4.6 %shard_map.111 = (bf16[8,176,128]{2,1,0:T(8,128)(2,1)}, bf16[8,176,128]{2,1,0:T(8,128)(2,1)}) custom-call(s32[2]{0:T(128)} %pad_add_fusion.refs_0_, bf16[4,128,512]{2,1,0:T(8,128)(2,1)} %bitcast.81, bf16[4,128,896]{2,1,0:T(8,128)(2,1)} %bitcast.63, f32[128,256]{1,0:T(8,128)} %all_gather.62.refs_1_.refs_6_.refs_3_, ...), custom_call_target="tpu_custom_call" | custom-call | tf_op jit(solution)/shard_map/pallas_call | solution.py:354
  280.0 1.9 collective-permute-done
  281.9 1.5 add_convert_fusion
  283.4 22.3 %all_to_all.20 = bf16[4,8,176,128]{3,2,1,0:T(8,128)(2,1)S(1)} all-to-all(bf16[4,8,176,128]{3,2,1,0:T(8,128)(2,1)S(1)} %add_convert_fusion), channel_id=1, replica_groups=mesh['y'=4,'z'=8,'x'=4,'c'=2] {'y'}, dimensions={0} | all-to-all | bytes 2883584 | tf_op jit(solution)/shard_map/all_to_all | solution.py:42
  306.0 19.1 %all_to_all.21 = bf16[8,176,128]{2,1,0:T(8,128)(2,1)S(1)} all-to-all(bf16[8,176,128]{2,1,0:T(8,128)(2,1)S(1)} %reduce_sum.51), channel_id=1, replica_groups=mesh['y'=4,'z'=8,'x'=4,'c'=2] {'z'}, dimensions={0} | all-to-all | bytes 720896 | tf_op jit(solution)/shard_map/all_to_all | solution.py:42
  (50 shorter events, 13.1 us)
Async XLA Ops:
  7.2 117.0 %all-gather.11.cloned.1.call-start = ((), (), s32[]{:S(2)}) async-start(), calls=%async_computation.4 | async-start | bytes 17039360 | tf_op jit(solution)/shard_map/all_gather | solution.py:224
  14.1 18.6 %all-to-all-start = ((bf16[4,2,32,2048]{3,2,1,0:T(8,128)(2,1)}), bf16[4,2,32,2048]{3,2,1,0:T(8,128)(2,1)}, u32[]{:S(2)}, u32[]{:S(2)}) async-start(bf16[4,2,32,2048]{3,2,1,0:T(8,128)(2,1)} %reshape.50), calls=%async_computation | async-start | bytes 2097152 | tf_op jit(solution)/shard_map/all_to_all | solution.py:42
  34.6 4.8 %copy-start.6 = (s32[2,2]{1,0:T(2,128)S(1)}, s32[2,2]{1,0:T(2,128)}, u32[]{:S(2)}) copy-start(s32[2,2]{1,0:T(2,128)} %param.16) | copy-start | bytes 52
  34.6 5.5 %copy-start.5 = (s32[4]{0:T(128)S(1)}, s32[4]{0:T(128)}, u32[]{:S(2)}) copy-start(s32[4]{0:T(128)} %param.17) | copy-start | bytes 52
  34.6 8.1 %copy-start.4 = (f32[1,8192]{1,0:T(1,128)S(1)}, f32[1,8192]{1,0:T(1,128)}, u32[]{:S(2)}) copy-start(f32[1,8192]{1,0:T(1,128)} %param.15) | copy-start | bytes 98308
  34.6 8.9 %copy-start.3 = (bf16[1,160,512]{2,1,0:T(8,128)(2,1)S(1)}, bf16[1,160,512]{2,1,0:T(8,128)(2,1)}, u32[]{:S(2)}) copy-start(bf16[1,160,512]{2,1,0:T(8,128)(2,1)} %param.14) | copy-start | bytes 491524
  34.6 82.7 %all-to-all-start.1 = ((bf16[4,160,2048]{2,1,0:T(8,128)(2,1)}), bf16[4,160,2048]{2,1,0:T(8,128)(2,1)S(1)}, u32[]{:S(2)}, u32[]{:S(2)}) async-start(bf16[4,160,2048]{2,1,0:T(8,128)(2,1)} %broadcast_in_dim.49), calls=%async_computation.1 | async-start | bytes 5242880 | tf_op jit(solution)/shard_map/all_to_all | solution.py:42
  218.0 62.0 %collective-permute-start.3 = (bf16[8,176,128]{2,1,0:T(8,128)(2,1)}, bf16[8,176,128]{2,1,0:T(8,128)(2,1)S(1)}, u32[]{:S(2)}, u32[]{:S(2)}) collective-permute-start(bf16[8,176,128]{2,1,0:T(8,128)(2,1)} %get-tuple-element.51), channel_id=1, source_target_pairs={{0,1},{1,0},{2,3},{3,2},{4,5},{5,4},{6,7},{7,6},{8,9},{9,8},{10,11... | collective-permute-start | bytes 1081352 | tf_op jit(solution)/shard_map/ppermute | solution.py:364
  239.5 40.5 %collective-permute-start.2 = (bf16[8,176,128]{2,1,0:T(8,128)(2,1)}, bf16[8,176,128]{2,1,0:T(8,128)(2,1)S(1)}, u32[]{:S(2)}, u32[]{:S(2)}) collective-permute-start(bf16[8,176,128]{2,1,0:T(8,128)(2,1)} %get-tuple-element.50), channel_id=1, source_target_pairs={{0,1},{1,0},{2,3},{3,2},{4,5},{5,4},{6,7},{7,6},{8,9},{9,8},{10,11... | collective-permute-start | bytes 1081352 | tf_op jit(solution)/shard_map/ppermute | solution.py:364
  261.1 18.9 %collective-permute-start.1 = (bf16[8,176,128]{2,1,0:T(8,128)(2,1)}, bf16[8,176,128]{2,1,0:T(8,128)(2,1)S(1)}, u32[]{:S(2)}, u32[]{:S(2)}) collective-permute-start(bf16[8,176,128]{2,1,0:T(8,128)(2,1)} %get-tuple-element.49), channel_id=1, source_target_pairs={{0,1},{1,0},{2,3},{3,2},{4,5},{5,4},{6,7},{7,6},{8,9},{9,8},{10,11... | collective-permute-start | bytes 1081352 | tf_op jit(solution)/shard_map/ppermute | solution.py:364
  275.4 6.5 %copy-start = (bf16[8,176,128]{2,1,0:T(8,128)(2,1)S(1)}, bf16[8,176,128]{2,1,0:T(8,128)(2,1)}, u32[]{:S(2)}) copy-start(bf16[8,176,128]{2,1,0:T(8,128)(2,1)} %get-tuple-element.47) | copy-start | bytes 1081348
  275.4 6.5 %copy-start.1 = (bf16[8,176,128]{2,1,0:T(8,128)(2,1)S(1)}, bf16[8,176,128]{2,1,0:T(8,128)(2,1)}, u32[]{:S(2)}) copy-start(bf16[8,176,128]{2,1,0:T(8,128)(2,1)} %get-tuple-element.46) | copy-start | bytes 1081348
  275.4 6.5 %copy-start.2 = (bf16[8,176,128]{2,1,0:T(8,128)(2,1)S(1)}, bf16[8,176,128]{2,1,0:T(8,128)(2,1)}, u32[]{:S(2)}) copy-start(bf16[8,176,128]{2,1,0:T(8,128)(2,1)} %get-tuple-element.45) | copy-start | bytes 1081348
  280.0 1.9 collective-permute-start
Sparse Core Ops, SparseCore 0:
  10.7 113.4 all-gather.10

commit v2 on v1

--- a/solution.py
+++ b/solution.py
@@ -17,6 +17,7 @@
 LANES = 128
 STEP = 512
 INTERPRET = False
+KERNEL_BYTES = 50 * 1024 * 1024
 
 
 def contract(left, right, left_dim, right_dim):
@@ -57,8 +58,9 @@
     return total[:, :value_cols], side, lax.rsqrt(mean + EPSILON)
 
 
-def forward_kernel(*refs, first, sizes):
+def forward_kernel(*refs, layer, sizes):
     value_cols, chunk, packed, width = sizes
+    first = layer == 0
     if first:
         grad, last_out, state, value_w, down_w, gain, sent, last_sum, scaled = refs[:9]
         acc, side_acc, square_acc, last_acc = refs[9:]
@@ -78,7 +80,7 @@
         else:
             value_part, side, inv = token_stats(before, value_cols, chunk, packed, width)
             low = (side * inv * coef[...]).astype(BF)
-            values[...] = (value_part * inv + contract(low, up[0], 1, 0)).astype(BF)
+            values[...] = (value_part * inv + contract(low, up[layer - 1], 1, 0)).astype(BF)
 
     if first:
         wide = state[...].astype(F32)
@@ -101,7 +103,9 @@
             last_sum[...] = last
             sent[:, value_cols : value_cols + chunk] = last[:, :chunk]
         else:
-            sent[:, value_cols : value_cols + chunk] = last_piece[...]
+            sent[:, value_cols : value_cols + chunk] = last_piece[
+                :, layer * chunk : (layer + 1) * chunk
+            ]
         squares = square_acc[:, :1]
         high = squares.astype(BF).astype(F32)
         lane = lax.broadcasted_iota(jnp.int32, side_acc.shape, 1)
@@ -110,8 +114,9 @@
         sent[:, value_cols + chunk :] = side.astype(BF)
 
 
-def backward_kernel(*refs, last, bottom, sizes, spots):
+def backward_kernel(*refs, layer, last, sizes, spots):
     value_cols, chunk, packed, width = sizes
+    bottom = layer == 0
     nz, nx, nc, each = spots
     refs = list(refs)
     take = lambda n: [refs.pop(0) for _ in range(n)]
@@ -131,11 +136,15 @@
 
     @pl.when(step == 0)
     def _():
-        summed_pieces = [piece[...].astype(F32).sum(axis=0) for piece in pieces]
+        first = value_cols if last else 0
+        wide = chunk if last else value_cols
+        summed_pieces = [
+            piece[:, :, first : first + wide].astype(F32).sum(axis=0) for piece in pieces
+        ]
         total = summed_pieces[0] if len(pieces) == 1 else jnp.concatenate(summed_pieces, axis=1)
         value_grad = total.astype(BF)
         wide_value = value_grad.astype(F32)
-        low_grad = (contract(value_grad, up[0], 1, 1) * coef[...]).astype(BF)
+        low_grad = (contract(value_grad, up[layer], 1, 1) * coef[...]).astype(BF)
         wide_low = low_grad.astype(F32)
         value_part, side, inv = token_stats(before, value_cols, chunk, packed, width)
         mixed_low[...] = (wide_low * inv).astype(BF)
@@ -177,8 +186,8 @@
             sent[...] = acc[...].astype(BF)
 
 
-def whole(shape):
-    return pl.BlockSpec(shape, lambda i: (0,) * len(shape))
+def whole():
+    return pl.BlockSpec(memory_space=pltpu.VMEM)
 
 
 def columns(tokens):
@@ -187,10 +196,6 @@
 
 def weight(layer, half, cols):
     return pl.BlockSpec((1, STEP, cols), lambda i: (layer, i, half))
-
-
-def layered(layer, shape):
-    return pl.BlockSpec((1,) + shape, lambda i: (layer,) + (0,) * len(shape))
 
 
 def along(layer, rows):
@@ -239,20 +244,30 @@
     state = spread[:, 0].reshape(nx * tokens, depth)
     grad = spread[:, 1].reshape(nx * tokens, depth)
 
-    down_local = lax.dynamic_index_in_dim(
-        adapter_down_weight[0].T.reshape(packed, nz, nx, lanes), xi, 2, keepdims=False
-    ).reshape(1, packed, depth)
-    downs_full = exchanged(jnp.broadcast_to(down_local, (layers, packed, depth)), "y")
     padded = -(-packed // LANES) * LANES
-    downs_full = jnp.pad(downs_full, ((0, 0), (0, padded - packed), (0, 0)))
-
-    gains_local = lax.dynamic_index_in_dim(
+    half = packed // nc
+    down_half = lax.dynamic_slice(
+        adapter_down_weight[0].T.reshape(packed, nz, nx, lanes),
+        (ci * half, 0, xi, 0),
+        (half, nz, 1, lanes),
+    ).reshape(1, half, depth)
+    mine = exchanged(jnp.broadcast_to(down_half, (layers, half, depth)), "y")
+    theirs = lax.ppermute(mine, "c", [(j, 1 - j) for j in range(nc)])
+    ordered = [jnp.where(ci == 0, mine, theirs), jnp.where(ci == 0, theirs, mine)]
+    filler = jnp.zeros((layers, padded - packed, depth), BF)
+    downs_full = jnp.concatenate(ordered + [filler], axis=1)
+
+    gain_own = lax.dynamic_index_in_dim(
         input_norm_scale.reshape(nz, nx, lanes), xi, 1, keepdims=False
-    ).reshape(depth)
-    gains = lax.all_gather(gains_local, "y", axis=0, tiled=False)
-    gains = gains.reshape(layers, 1, depth)
-    ups = lax.all_gather(adapter_up_weight[0], "y", axis=0, tiled=False)
-    ups = jnp.pad(ups, ((0, 0), (0, padded - packed), (0, 0)))
+    ).reshape(depth // value_cols, value_cols)
+    high = lax.reduce_precision(gain_own, 8, 7)
+    middle = lax.reduce_precision(gain_own - high, 8, 7)
+    parts = [high, middle, gain_own - high - middle]
+    small = jnp.concatenate([adapter_up_weight[0]] + [part.astype(BF) for part in parts], axis=0)
+    small = lax.all_gather(small, "y", axis=0, tiled=False)
+    ups = jnp.pad(small[:, :packed], ((0, 0), (0, padded - packed), (0, 0)))
+    gains = small[:, packed:].astype(F32).reshape(layers, 3, 1, depth)
+    gains = gains[:, 0] + gains[:, 1] + gains[:, 2]
     adapter = lax.dynamic_index_in_dim(segment_adapter_index.reshape(ny), yi, 0, keepdims=False)
     coef_row = coefficient_row(adapter, adapter_rank_blocks, packed, padded)
     coef = lax.all_gather(
@@ -266,7 +281,12 @@
     each = value_cols // (nz * nx * nc)
     steps = depth // STEP
     shape = jax.ShapeDtypeStruct
-    call = functools.partial(pl.pallas_call, grid=(steps,), interpret=INTERPRET)
+    call = functools.partial(
+        pl.pallas_call,
+        grid=(steps,),
+        interpret=INTERPRET,
+        compiler_params=pltpu.CompilerParams(vmem_limit_bytes=KERNEL_BYTES),
+    )
     sent_shape, wide_shape = shape((count, wire), BF), shape((count, depth), BF)
     sums = [
         pltpu.VMEM((count, value_cols), F32),
@@ -276,7 +296,7 @@
     top = layers - 1
 
     sent, last, scaled_input = call(
-        functools.partial(forward_kernel, first=True, sizes=sizes),
+        functools.partial(forward_kernel, layer=0, sizes=sizes),
         out_shape=(sent_shape, shape((count, value_cols), BF), wide_shape),
         in_specs=[
             columns(count),
@@ -286,26 +306,26 @@
             along(0, padded),
             along(0, 1),
         ],
-        out_specs=(whole((count, wire)), whole((count, value_cols)), columns(count)),
+        out_specs=(whole(), whole(), columns(count)),
         scratch_shapes=sums + [pltpu.VMEM((count, value_cols), F32)],
     )(grad, full, state, full, downs_full, gains)
     arrived, inputs, scaled = [gathered(sent)], [state], [scaled_input]
     for layer in range(1, layers):
         sent, state, scaled_input = call(
-            functools.partial(forward_kernel, first=False, sizes=sizes),
+            functools.partial(forward_kernel, layer=layer, sizes=sizes),
             out_shape=(sent_shape, wide_shape, wide_shape),
             in_specs=[
-                whole((nx, count, wire)),
-                whole((count, padded)),
-                layered(layer - 1, (padded, value_cols)),
+                whole(),
+                whole(),
+                whole(),
                 columns(count),
                 weight(layer - 1, 1, value_cols),
                 weight(layer, 0, value_cols),
                 along(layer, padded),
                 along(layer, 1),
-                pl.BlockSpec((count, chunk), lambda i, layer=layer: (0, layer)),
+                whole(),
             ],
-            out_specs=(whole((count, wire)), columns(count), columns(count)),
+            out_specs=(whole(), columns(count), columns(count)),
             scratch_shapes=sums + [pltpu.VMEM((count, value_cols), BF)],
         )(arrived[-1], coef, ups, state, full, full, downs_full, gains, last)
         arrived.append(gathered(sent))
@@ -317,22 +337,20 @@
     block_rows = packed + each * (padded // LANES)
     block_shape = (nz, block_rows, LANES)
     kept, crossed = [None] * layers, [None] * layers
-    pieces, piece_specs = arrived, [
-        pl.BlockSpec((nx, count, chunk), lambda i: (0, 0, value_cols // chunk))
-    ] * layers
+    pieces = arrived
     for layer in reversed(range(layers)):
         bottom = layer == 0
         operands = [place_ids, *pieces, arrived[layer], coef, ups, scaled[layer]]
         specs = [
             pl.BlockSpec(memory_space=pltpu.SMEM),
-            *piece_specs,
-            whole((nx, count, wire)),
-            whole((count, padded)),
-            layered(layer, (padded, value_cols)),
+            *[whole() for _ in pieces],
+            whole(),
+            whole(),
+            whole(),
             columns(count),
         ]
         outs = [shape(block_shape, BF)] * 2
-        out_specs = [whole(block_shape)] * 2
+        out_specs = [whole()] * 2
         scratch = [pltpu.VMEM((count, padded), BF), pltpu.VMEM((value_cols, padded), F32)]
         if not bottom:
             operands += [inputs[layer], grad, full, downs_full, gains, full]
@@ -345,7 +363,7 @@
                 weight(layer - 1, 1, value_cols),
             ]
             outs += [shape((count, value_cols), BF), wide_shape]
-            out_specs += [whole((count, value_cols)), columns(count)]
+            out_specs += [whole(), columns(count)]
             scratch += [
                 pltpu.VMEM((count, value_cols), BF),
                 pltpu.VMEM((count, LANES), F32),
@@ -353,7 +371,7 @@
             ]
         results = call(
             functools.partial(
-                backward_kernel, last=layer == top, bottom=bottom, sizes=sizes, spots=spots
+                backward_kernel, layer=layer, last=layer == top, sizes=sizes, spots=spots
             ),
             out_shape=outs,
             in_specs=specs,
@@ -365,7 +383,6 @@
         if not bottom:
             grad = results[3]
             pieces = [gathered(results[2])]
-            piece_specs = [whole((nx, count, value_cols))]
 
     total = (jnp.stack(kept).astype(F32) + jnp.stack(crossed).astype(F32)).astype(BF)
     total = summed(exchanged(total, "y")).astype(BF)

time: 334 us -> 305 us (0.913)
  blocking collectives: 214 us -> 181 us
  waiting for transfers between devices: 10.2 us -> 30.3 us
  Pallas kernels: 52.1 us -> 42 us
  local copies, waits for them, and re-layouts: 22.4 us -> 14.5 us
  other arithmetic: 8.31 us -> 12 us
    all_gather x2 -> x1, blocking collectives: 57.2 us -> 27.6 us  [local(): small = lax.all_gather(small, 'y', axis=0, tiled=False)]
    all_gather x1, waiting for transfers between devices: 4.48 us -> 28.6 us  [local(): full = lax.all_gather(joined, GROUP, axis=0, tiled=False)]
    pallas_call x8, Pallas kernels: 52.1 us -> 42 us  [the longest x4 21.7 us: local(): call(functools.partial(backward_kernel, layer=layer, last=layer == top, s...]
    all_gather x7, blocking collectives: 103 us -> 97.6 us  [gathered(): return lax.all_gather(partial, 'x', axis=0, tiled=False)]
    all_to_all x2, waiting for transfers between devices: 3.8 us -> 0.01 us  [exchanged(): return lax.all_to_all(value, axis, split_axis=0, concat_axis=0, tiled=True)]
    all_gather x1, blocking collectives: 11.8 us -> 15.5 us  [local(): lax.all_gather(jnp.broadcast_to(coef_row, (tokens, padded)), 'x', axis=0,...]
    pad x2 -> x1, local copies, waits for them, and re-layouts: 3.45 us -> 0.08 us  [local(): ups = jnp.pad(small[:, :packed], ((0, 0), (0, padded - packed), (0, 0)))]
  transfers between devices with their start and end apart: 7 -> 8, of which waited for: 3 -> 2; matrix products, arithmetic and copies ran while one was open for 7% -> 7% of each run, Pallas kernels for 6% -> 5%
where the time goes in v2:
time: 305 us; the launch traced here: 304 us
  blocking collectives  181 us (59%)
  Pallas kernels  42 us (14%)
  waiting for transfers between devices  30.3 us (10%)
  between operations  15.1 us (5%)
  local copies, waits for them, and re-layouts  14.5 us (5%)
  other arithmetic  12 us (4%)
  starting transfers between devices  9.76 us (3%)
    all_gather x7, blocking collectives, gathered(): return lax.all_gather(partial, 'x', axis=0, tiled=False)  97.6 us
    all_to_all x2, blocking collectives, exchanged(): return lax.all_to_all(value, axis, split_axis=0, concat_axis=0, tiled=True)  40 us
    all_gather x1, waiting for transfers between devices, local(): full = lax.all_gather(joined, GROUP, axis=0, tiled=False)  28.6 us
    all_gather x1, blocking collectives, local(): small = lax.all_gather(small, 'y', axis=0, tiled=False)  27.6 us
    pallas_call x4, Pallas kernels, local(): call(functools.partial(backward_kernel, layer=layer, last=layer == top, s...  21.7 us
    pallas_call x3, Pallas kernels, local(): call(functools.partial(forward_kernel, layer=layer, sizes=sizes), out_sha...  16.2 us
    all_gather x1, blocking collectives, local(): lax.all_gather(jnp.broadcast_to(coef_row, (tokens, padded)), 'x', axis=0,...  15.5 us
    all_to_all x2, starting transfers between devices, exchanged(): return lax.all_to_all(value, axis, split_axis=0, concat_axis=0, tiled=True)  9.44 us
  transfers between devices with their start and end apart: 8, of which 2 were waited for; matrix products, arithmetic and copies ran while one was open for 7% of the time, Pallas kernels for 5%

profile of v2, /device:TPU:2, one launch (start us, length us, event | category | flops | bytes accessed | tf_op | source)
XLA Modules:
  0.0 304.2 jit_solution(15817407251749119290)
XLA Ops:
  8.2 1.6 pad_maximum_fusion
  9.9 4.3 %reshape.91 = bf16[160,8,4,256]{3,2,1,0:T(4,128)(2,1)S(1)} reshape(bf16[160,8192]{1,0:T(8,128)(2,1)} %bitcast.88) | data formatting | bytes 5242880 | tf_op jit(solution)/shard_map/reshape | solution.py:250
  14.2 1.9 dynamic-slice_reduce_fusion
  16.2 1.2 broadcast_in_dim.52
  17.5 4.6 %all-to-all-start.1 = ((bf16[4,80,2048]{2,1,0:T(8,128)(2,1)}), bf16[4,80,2048]{2,1,0:T(8,128)(2,1)}, u32[]{:S(2)}, u32[]{:S(2)}) async-start(bf16[4,80,2048]{2,1,0:T(8,128)(2,1)} %broadcast_in_dim.52), calls=%async_computation.1 | async-start | bytes 2621440 | tf_op jit(solution)/shard_map/all_to_all | solution.py:43
  22.8 1.2 fusion.3
  26.0 27.6 %all-gather.9 = bf16[4,172,512]{2,1,0:T(8,128)(2,1)S(1)} all-gather(bf16[1,172,512]{2,1,0:T(8,128)(2,1)S(1)} %maximum_bitcast_fusion.1), channel_id=3, replica_groups=mesh['y'=4,'z'=8,'x'=4,'c'=2] {'y'}, dimensions={0}, use_global_device_ids=true | all-gather | bytes 880640 | tf_op jit(solution)/shard_map/all_gather | solution.py:267
  53.7 1.5 constant_dynamic-slice_fusion
  56.8 1.3 reshape.89
  58.6 4.8 %all-to-all-start = ((bf16[4,2,32,2048]{3,2,1,0:T(8,128)(2,1)}), bf16[4,2,32,2048]{3,2,1,0:T(8,128)(2,1)S(1)}, u32[]{:S(2)}, u32[]{:S(2)}) async-start(bf16[4,2,32,2048]{3,2,1,0:T(8,128)(2,1)} %reshape.89), calls=%async_computation | async-start | bytes 2097152 | tf_op jit(solution)/shard_map/all_to_all | solution.py:43
  64.1 15.5 %all_gather.63.refs_1_.refs_6_.refs_3_ = f32[128,256]{1,0:T(8,128)S(1)} all-gather(f32[32,256]{1,0:T(8,128)S(1)} %broadcast_in_dim.59), channel_id=1, replica_groups=mesh['y'=4,'z'=8,'x'=4,'c'=2] {'x'}, dimensions={0}, use_global_device_ids=true | all-gather | bytes 163840 | tf_op jit(solution)/shard_map/all_gather | solution.py:273
  79.8 2.3 broadcast_select_fusion.1
  82.1 2.9 maximum_maximum_fusion.refs_4_.refs_6_.refs_12_.refs_9_
  85.0 28.6 %all-gather.12.cloned.1.call-done = bf16[8192,1024]{1,0:T(8,128)(2,1)} async-done(((bf16[128,1024]{1,0:T(8,128)(2,1)}), bf16[8192,1024]{1,0:T(8,128)(2,1)}) %all-gather.12.cloned.1.call-update) | async-done | bytes 16777232 | tf_op jit(solution)/shard_map/all_gather | solution.py:229
  113.6 4.1 %shard_map.104 = (bf16[128,896]{1,0:T(8,128)(2,1)S(1)}, bf16[128,512]{1,0:T(8,128)(2,1)S(1)}, bf16[128,2048]{1,0:T(8,128)(2,1)S(1)}) custom-call(bf16[128,2048]{1,0:T(8,128)(2,1)S(1)} %bitcast.63, bf16[4,2048,1024]{2,1,0:T(8,128)(2,1)} %bitcast.72, bf16[128,2048]{1,0:T(8,128)(2,1)S(1)} %bitcast.61, bf16[4,2048,1024]{2,1,0:T(8,128)(2,1)} %bitcast.73, ...), custom_call_target="tpu_custom_call" | custom-call | tf_op jit(solution)/shard_map/pallas_call | solution.py:298
  117.7 15.0 %all-gather.2 = bf16[512,896]{1,0:T(8,128)(2,1)S(1)} all-gather(bf16[128,896]{1,0:T(8,128)(2,1)S(1)} %get-tuple-element.27), channel_id=4, replica_groups=mesh['y'=4,'z'=8,'x'=4,'c'=2] {'x'}, dimensions={0}, use_global_device_ids=true | all-gather | bytes 1146880 | tf_op jit(solution)/shard_map/all_gather | solution.py:51
  132.7 5.2 %shard_map.105 = (bf16[128,896]{1,0:T(8,128)(2,1)S(1)}, bf16[128,2048]{1,0:T(8,128)(2,1)S(1)}, bf16[128,2048]{1,0:T(8,128)(2,1)S(1)}) custom-call(bf16[4,128,896]{2,1,0:T(8,128)(2,1)S(1)} %bitcast.52, f32[128,256]{1,0:T(8,128)S(1)} %all_gather.63.refs_1_.refs_6_.refs_3_, bf16[4,256,512]{2,1,0:T(8,128)(2,1)S(1)} %pad.4.refs_2_.refs_7_.refs_4_, ...), custom_call_target="tpu_custom_call" | custom-call | tf_op jit(solution)/shard_map/pallas_call | solution.py:314
  137.9 13.6 %all-gather.3 = bf16[512,896]{1,0:T(8,128)(2,1)S(1)} all-gather(bf16[128,896]{1,0:T(8,128)(2,1)S(1)} %get-tuple-element.29), channel_id=5, replica_groups=mesh['y'=4,'z'=8,'x'=4,'c'=2] {'x'}, dimensions={0}, use_global_device_ids=true | all-gather | bytes 1146880 | tf_op jit(solution)/shard_map/all_gather | solution.py:51
  151.5 5.5 %shard_map.106 = (bf16[128,896]{1,0:T(8,128)(2,1)S(1)}, bf16[128,2048]{1,0:T(8,128)(2,1)S(1)}, bf16[128,2048]{1,0:T(8,128)(2,1)S(1)}) custom-call(bf16[4,128,896]{2,1,0:T(8,128)(2,1)S(1)} %bitcast.55, f32[128,256]{1,0:T(8,128)S(1)} %all_gather.63.refs_1_.refs_6_.refs_3_, bf16[4,256,512]{2,1,0:T(8,128)(2,1)S(1)} %pad.4.refs_2_.refs_7_.refs_4_, ...), custom_call_target="tpu_custom_call" | custom-call | tf_op jit(solution)/shard_map/pallas_call | solution.py:314
  157.0 14.3 %all-gather.4 = bf16[512,896]{1,0:T(8,128)(2,1)S(1)} all-gather(bf16[128,896]{1,0:T(8,128)(2,1)S(1)} %get-tuple-element.31), channel_id=6, replica_groups=mesh['y'=4,'z'=8,'x'=4,'c'=2] {'x'}, dimensions={0}, use_global_device_ids=true | all-gather | bytes 1146880 | tf_op jit(solution)/shard_map/all_gather | solution.py:51
  171.3 5.5 %shard_map.107 = (bf16[128,896]{1,0:T(8,128)(2,1)S(1)}, bf16[128,2048]{1,0:T(8,128)(2,1)S(1)}, bf16[128,2048]{1,0:T(8,128)(2,1)S(1)}) custom-call(bf16[4,128,896]{2,1,0:T(8,128)(2,1)S(1)} %bitcast.58, f32[128,256]{1,0:T(8,128)S(1)} %all_gather.63.refs_1_.refs_6_.refs_3_, bf16[4,256,512]{2,1,0:T(8,128)(2,1)S(1)} %pad.4.refs_2_.refs_7_.refs_4_, ...), custom_call_target="tpu_custom_call" | custom-call | tf_op jit(solution)/shard_map/pallas_call | solution.py:314
  176.9 14.3 %all-gather.5 = bf16[512,896]{1,0:T(8,128)(2,1)} all-gather(bf16[128,896]{1,0:T(8,128)(2,1)S(1)} %get-tuple-element.33), channel_id=7, replica_groups=mesh['y'=4,'z'=8,'x'=4,'c'=2] {'x'}, dimensions={0}, use_global_device_ids=true | all-gather | bytes 1146880 | tf_op jit(solution)/shard_map/all_gather | solution.py:51
  191.2 7.0 %shard_map.108 = (bf16[8,176,128]{2,1,0:T(8,128)(2,1)S(1)}, bf16[8,176,128]{2,1,0:T(8,128)(2,1)S(1)}, bf16[128,512]{1,0:T(8,128)(2,1)S(1)}, bf16[128,2048]{1,0:T(8,128)(2,1)S(1)}) custom-call(s32[2]{0:T(128)S(1)} %pad_add_fusion.refs_0_, bf16[4,128,896]{2,1,0:T(8,128)(2,1)S(1)} %bitcast.53, bf16[4,128,896]{2,1,0:T(8,128)(2,1)} %bitcast.56, ...), custom_call_target="tpu_custom_call" | custom-call | tf_op jit(solution)/shard_map/pallas_call | solution.py:372
  198.3 13.4 %all-gather.6 = bf16[512,512]{1,0:T(8,128)(2,1)S(1)} all-gather(bf16[128,512]{1,0:T(8,128)(2,1)S(1)} %get-tuple-element.36), channel_id=8, replica_groups=mesh['y'=4,'z'=8,'x'=4,'c'=2] {'x'}, dimensions={0}, use_global_device_ids=true | all-gather | bytes 655360 | tf_op jit(solution)/shard_map/all_gather | solution.py:51
  211.7 5.9 %shard_map.109 = (bf16[8,176,128]{2,1,0:T(8,128)(2,1)S(1)}, bf16[8,176,128]{2,1,0:T(8,128)(2,1)S(1)}, bf16[128,512]{1,0:T(8,128)(2,1)S(1)}, bf16[128,2048]{1,0:T(8,128)(2,1)S(1)}) custom-call(s32[2]{0:T(128)S(1)} %pad_add_fusion.refs_0_, bf16[4,128,512]{2,1,0:T(8,128)(2,1)S(1)} %bitcast.66, bf16[4,128,896]{2,1,0:T(8,128)(2,1)} %bitcast.60, ...), custom_call_target="tpu_custom_call" | custom-call | tf_op jit(solution)/shard_map/pallas_call | solution.py:372
  217.7 13.4 %all-gather.7 = bf16[512,512]{1,0:T(8,128)(2,1)S(1)} all-gather(bf16[128,512]{1,0:T(8,128)(2,1)S(1)} %get-tuple-element.39), channel_id=9, replica_groups=mesh['y'=4,'z'=8,'x'=4,'c'=2] {'x'}, dimensions={0}, use_global_device_ids=true | all-gather | bytes 655360 | tf_op jit(solution)/shard_map/all_gather | solution.py:51
  231.1 6.6 %shard_map.110 = (bf16[8,176,128]{2,1,0:T(8,128)(2,1)S(1)}, bf16[8,176,128]{2,1,0:T(8,128)(2,1)S(1)}, bf16[128,512]{1,0:T(8,128)(2,1)S(1)}, bf16[128,2048]{1,0:T(8,128)(2,1)}) custom-call(s32[2]{0:T(128)S(1)} %pad_add_fusion.refs_0_, bf16[4,128,512]{2,1,0:T(8,128)(2,1)S(1)} %bitcast.65, bf16[4,128,896]{2,1,0:T(8,128)(2,1)} %bitcast.57, ...), custom_call_target="tpu_custom_call" | custom-call | tf_op jit(solution)/shard_map/pallas_call | solution.py:372
  237.7 13.6 %all-gather.8 = bf16[512,512]{1,0:T(8,128)(2,1)S(1)} all-gather(bf16[128,512]{1,0:T(8,128)(2,1)S(1)} %get-tuple-element.42), channel_id=10, replica_groups=mesh['y'=4,'z'=8,'x'=4,'c'=2] {'x'}, dimensions={0}, use_global_device_ids=true | all-gather | bytes 655360 | tf_op jit(solution)/shard_map/all_gather | solution.py:51
  251.3 2.1 shard_map.111
  253.6 1.6 collective-permute-done.1
  255.8 22.3 %all_to_all.20 = bf16[4,8,176,128]{3,2,1,0:T(8,128)(2,1)S(1)} all-to-all(bf16[4,8,176,128]{3,2,1,0:T(8,128)(2,1)S(1)} %add_convert_fusion), channel_id=1, replica_groups=mesh['y'=4,'z'=8,'x'=4,'c'=2] {'y'}, dimensions={0} | all-to-all | bytes 2883584 | tf_op jit(solution)/shard_map/all_to_all | solution.py:43
  278.4 17.6 %all_to_all.21 = bf16[8,176,128]{2,1,0:T(8,128)(2,1)S(1)} all-to-all(bf16[8,176,128]{2,1,0:T(8,128)(2,1)S(1)} %reduce_sum.51), channel_id=1, replica_groups=mesh['y'=4,'z'=8,'x'=4,'c'=2] {'z'}, dimensions={0} | all-to-all | bytes 720896 | tf_op jit(solution)/shard_map/all_to_all | solution.py:43
  (66 shorter events, 8.5 us)
Async XLA Ops:
  7.2 106.4 %all-gather.12.cloned.1.call-start = ((), (), s32[]{:S(2)}) async-start(), calls=%async_computation.4 | async-start | bytes 17039360 | tf_op jit(solution)/shard_map/all_gather | solution.py:229
  17.4 4.6 %copy-start.8 = (s32[2,2]{1,0:T(2,128)S(1)}, s32[2,2]{1,0:T(2,128)}, u32[]{:S(2)}) copy-start(s32[2,2]{1,0:T(2,128)} %param.16) | copy-start | bytes 52
  17.4 5.3 %copy-start.7 = (s32[4]{0:T(128)S(1)}, s32[4]{0:T(128)}, u32[]{:S(2)}) copy-start(s32[4]{0:T(128)} %param.17) | copy-start | bytes 52
  17.4 7.7 %copy-start.6 = (f32[1,8192]{1,0:T(1,128)S(1)}, f32[1,8192]{1,0:T(1,128)}, u32[]{:S(2)}) copy-start(f32[1,8192]{1,0:T(1,128)} %param.15) | copy-start | bytes 98308
  17.5 8.5 %copy-start.5 = (bf16[1,160,512]{2,1,0:T(8,128)(2,1)S(1)}, bf16[1,160,512]{2,1,0:T(8,128)(2,1)}, u32[]{:S(2)}) copy-start(bf16[1,160,512]{2,1,0:T(8,128)(2,1)} %param.14) | copy-start | bytes 491524
  17.5 41.1 %all-to-all-start.1 = ((bf16[4,80,2048]{2,1,0:T(8,128)(2,1)}), bf16[4,80,2048]{2,1,0:T(8,128)(2,1)}, u32[]{:S(2)}, u32[]{:S(2)}) async-start(bf16[4,80,2048]{2,1,0:T(8,128)(2,1)} %broadcast_in_dim.52), calls=%async_computation.1 | async-start | bytes 2621440 | tf_op jit(solution)/shard_map/all_to_all | solution.py:43
  53.6 1.5 copy-start.4
  56.8 1.3 slice-start
  58.2 113.1 %copy-start = (bf16[4,256,512]{2,1,0:T(8,128)(2,1)}, bf16[4,256,512]{2,1,0:T(8,128)(2,1)S(1)}, u32[]{:S(2)}) copy-start(bf16[4,256,512]{2,1,0:T(8,128)(2,1)S(1)} %pad.4.refs_2_.refs_7_.refs_4_) | copy-start | bytes 3145732
  58.6 21.1 %all-to-all-start = ((bf16[4,2,32,2048]{3,2,1,0:T(8,128)(2,1)}), bf16[4,2,32,2048]{3,2,1,0:T(8,128)(2,1)S(1)}, u32[]{:S(2)}, u32[]{:S(2)}) async-start(bf16[4,2,32,2048]{3,2,1,0:T(8,128)(2,1)} %reshape.89), calls=%async_computation | async-start | bytes 2097152 | tf_op jit(solution)/shard_map/all_to_all | solution.py:43
  63.4 16.4 %collective-permute-start = (bf16[4,80,2048]{2,1,0:T(8,128)(2,1)}, bf16[4,80,2048]{2,1,0:T(8,128)(2,1)}, u32[]{:S(2)}, u32[]{:S(2)}) collective-permute-start(bf16[4,80,2048]{2,1,0:T(8,128)(2,1)} %all-to-all-done.1), channel_id=1, source_target_pairs={{0,1},{1,0},{2,3},{3,2},{4,5},{5,4},{6,7},{7,6},{8,9},{9,8},{10,11... | collective-permute-start | bytes 3932168 | tf_op jit(solution)/shard_map/ppermute | solution.py:255
  151.5 5.5 %copy-start.2 = (bf16[512,896]{1,0:T(8,128)(2,1)}, bf16[512,896]{1,0:T(8,128)(2,1)S(1)}, u32[]{:S(2)}) copy-start(bf16[512,896]{1,0:T(8,128)(2,1)S(1)} %all-gather.3) | copy-start | bytes 2752516
  171.3 5.5 %copy-start.3 = (bf16[512,896]{1,0:T(8,128)(2,1)}, bf16[512,896]{1,0:T(8,128)(2,1)S(1)}, u32[]{:S(2)}) copy-start(bf16[512,896]{1,0:T(8,128)(2,1)S(1)} %all-gather.4) | copy-start | bytes 2752516
  198.2 55.3 %collective-permute-start.4 = (bf16[8,176,128]{2,1,0:T(8,128)(2,1)S(1)}, bf16[8,176,128]{2,1,0:T(8,128)(2,1)S(1)}, u32[]{:S(2)}, u32[]{:S(2)}) collective-permute-start(bf16[8,176,128]{2,1,0:T(8,128)(2,1)S(1)} %get-tuple-element.51), channel_id=1, source_target_pairs={{0,1},{1,0},{2,3},{3,2},{4,5},{5,4},{6,7},{7,6},{8,9},{9,8},{10,11... | collective-permute-start | bytes 1081352 | tf_op jit(solution)/shard_map/ppermute | solution.py:382
  217.6 35.9 %collective-permute-start.3 = (bf16[8,176,128]{2,1,0:T(8,128)(2,1)S(1)}, bf16[8,176,128]{2,1,0:T(8,128)(2,1)S(1)}, u32[]{:S(2)}, u32[]{:S(2)}) collective-permute-start(bf16[8,176,128]{2,1,0:T(8,128)(2,1)S(1)} %get-tuple-element.50), channel_id=1, source_target_pairs={{0,1},{1,0},{2,3},{3,2},{4,5},{5,4},{6,7},{7,6},{8,9},{9,8},{10,11... | collective-permute-start | bytes 1081352 | tf_op jit(solution)/shard_map/ppermute | solution.py:382
  231.1 20.2 %copy-start.1 = (bf16[4,256,512]{2,1,0:T(8,128)(2,1)S(1)}, bf16[4,256,512]{2,1,0:T(8,128)(2,1)}, u32[]{:S(2)}) copy-start(bf16[4,256,512]{2,1,0:T(8,128)(2,1)} %copy-done) | copy-start | bytes 3145732
  237.7 15.8 %collective-permute-start.2 = (bf16[8,176,128]{2,1,0:T(8,128)(2,1)S(1)}, bf16[8,176,128]{2,1,0:T(8,128)(2,1)S(1)}, u32[]{:S(2)}, u32[]{:S(2)}) collective-permute-start(bf16[8,176,128]{2,1,0:T(8,128)(2,1)S(1)} %get-tuple-element.49), channel_id=1, source_target_pairs={{0,1},{1,0},{2,3},{3,2},{4,5},{5,4},{6,7},{7,6},{8,9},{9,8},{10,11... | collective-permute-start | bytes 1081352 | tf_op jit(solution)/shard_map/ppermute | solution.py:382
  253.4 1.8 collective-permute-start.1
Sparse Core Ops, SparseCore 0:
  10.7 102.8 all-gather.11

commit v3 on v2

--- a/solution.py
+++ b/solution.py
@@ -15,7 +15,7 @@
 F32 = jnp.float32
 GROUP = ("y", "z", "c")
 LANES = 128
-STEP = 512
+STEP = 1024
 INTERPRET = False
 KERNEL_BYTES = 50 * 1024 * 1024
 

time: 305 us -> 297 us (0.974)
  Pallas kernels: 42 us -> 35.4 us
  transfers between devices with their start and end apart: 8 -> 8, of which waited for: 2 -> 2; matrix products, arithmetic and copies ran while one was open for 7% -> 7% of each run, Pallas kernels for 5% -> 4%
where the time goes in v3:
time: 297 us
  blocking collectives  180 us (61%)
  Pallas kernels  35.4 us (12%)
  waiting for transfers between devices  30.3 us (10%)
  between operations  15.1 us (5%)
  local copies, waits for them, and re-layouts  14.5 us (5%)
  other arithmetic  12 us (4%)
  starting transfers between devices  9.76 us (3%)
    all_gather x7, blocking collectives, gathered(): return lax.all_gather(partial, 'x', axis=0, tiled=False)  97.2 us
    all_to_all x2, blocking collectives, exchanged(): return lax.all_to_all(value, axis, split_axis=0, concat_axis=0, tiled=True)  39.5 us
    all_gather x1, waiting for transfers between devices, local(): full = lax.all_gather(joined, GROUP, axis=0, tiled=False)  28.6 us
    all_gather x1, blocking collectives, local(): small = lax.all_gather(small, 'y', axis=0, tiled=False)  27.6 us
    pallas_call x4, Pallas kernels, local(): call(functools.partial(backward_kernel, layer=layer, last=layer == top, s...  18.8 us
    all_gather x1, blocking collectives, local(): lax.all_gather(jnp.broadcast_to(coef_row, (tokens, padded)), 'x', axis=0,...  15.5 us
    pallas_call x3, Pallas kernels, local(): call(functools.partial(forward_kernel, layer=layer, sizes=sizes), out_sha...  13.4 us
    all_to_all x2, starting transfers between devices, exchanged(): return lax.all_to_all(value, axis, split_axis=0, concat_axis=0, tiled=True)  9.44 us
  transfers between devices with their start and end apart: 8, of which 2 were waited for; matrix products, arithmetic and copies ran while one was open for 7% of the time, Pallas kernels for 4%

profile of v3, /device:TPU:2, one launch (start us, length us, event | category | flops | bytes accessed | tf_op | source)
XLA Modules:
  0.0 296.8 jit_solution(7525588027410618079)
XLA Ops:
  8.2 1.6 pad_maximum_fusion
  9.9 4.3 %reshape.91 = bf16[160,8,4,256]{3,2,1,0:T(4,128)(2,1)S(1)} reshape(bf16[160,8192]{1,0:T(8,128)(2,1)} %bitcast.88) | data formatting | bytes 5242880 | tf_op jit(solution)/shard_map/reshape | solution.py:250
  14.2 1.9 dynamic-slice_reduce_fusion
  16.2 1.2 broadcast_in_dim.52
  17.5 4.6 %all-to-all-start.1 = ((bf16[4,80,2048]{2,1,0:T(8,128)(2,1)}), bf16[4,80,2048]{2,1,0:T(8,128)(2,1)}, u32[]{:S(2)}, u32[]{:S(2)}) async-start(bf16[4,80,2048]{2,1,0:T(8,128)(2,1)} %broadcast_in_dim.52), calls=%async_computation.1 | async-start | bytes 2621440 | tf_op jit(solution)/shard_map/all_to_all | solution.py:43
  22.8 1.2 fusion.3
  26.0 27.6 %all-gather.9 = bf16[4,172,512]{2,1,0:T(8,128)(2,1)S(1)} all-gather(bf16[1,172,512]{2,1,0:T(8,128)(2,1)S(1)} %maximum_bitcast_fusion.1), channel_id=3, replica_groups=mesh['y'=4,'z'=8,'x'=4,'c'=2] {'y'}, dimensions={0}, use_global_device_ids=true | all-gather | bytes 880640 | tf_op jit(solution)/shard_map/all_gather | solution.py:267
  53.7 1.5 constant_dynamic-slice_fusion
  56.8 1.3 reshape.89
  58.6 4.8 %all-to-all-start = ((bf16[4,2,32,2048]{3,2,1,0:T(8,128)(2,1)}), bf16[4,2,32,2048]{3,2,1,0:T(8,128)(2,1)S(1)}, u32[]{:S(2)}, u32[]{:S(2)}) async-start(bf16[4,2,32,2048]{3,2,1,0:T(8,128)(2,1)} %reshape.89), calls=%async_computation | async-start | bytes 2097152 | tf_op jit(solution)/shard_map/all_to_all | solution.py:43
  64.1 15.5 %all_gather.63.refs_1_.refs_6_.refs_3_ = f32[128,256]{1,0:T(8,128)S(1)} all-gather(f32[32,256]{1,0:T(8,128)S(1)} %broadcast_in_dim.59), channel_id=1, replica_groups=mesh['y'=4,'z'=8,'x'=4,'c'=2] {'x'}, dimensions={0}, use_global_device_ids=true | all-gather | bytes 163840 | tf_op jit(solution)/shard_map/all_gather | solution.py:273
  79.8 2.3 broadcast_select_fusion.1
  82.1 2.9 maximum_maximum_fusion.refs_4_.refs_6_.refs_12_.refs_9_
  85.0 28.6 %all-gather.12.cloned.1.call-done = bf16[8192,1024]{1,0:T(8,128)(2,1)} async-done(((bf16[128,1024]{1,0:T(8,128)(2,1)}), bf16[8192,1024]{1,0:T(8,128)(2,1)}) %all-gather.12.cloned.1.call-update) | async-done | bytes 16777232 | tf_op jit(solution)/shard_map/all_gather | solution.py:229
  113.6 3.2 %shard_map.104 = (bf16[128,896]{1,0:T(8,128)(2,1)S(1)}, bf16[128,512]{1,0:T(8,128)(2,1)S(1)}, bf16[128,2048]{1,0:T(8,128)(2,1)S(1)}) custom-call(bf16[128,2048]{1,0:T(8,128)(2,1)S(1)} %bitcast.63, bf16[4,2048,1024]{2,1,0:T(8,128)(2,1)} %bitcast.72, bf16[128,2048]{1,0:T(8,128)(2,1)S(1)} %bitcast.61, bf16[4,2048,1024]{2,1,0:T(8,128)(2,1)} %bitcast.73, ...), custom_call_target="tpu_custom_call" | custom-call | tf_op jit(solution)/shard_map/pallas_call | solution.py:298
  116.9 15.0 %all-gather.2 = bf16[512,896]{1,0:T(8,128)(2,1)S(1)} all-gather(bf16[128,896]{1,0:T(8,128)(2,1)S(1)} %get-tuple-element.27), channel_id=4, replica_groups=mesh['y'=4,'z'=8,'x'=4,'c'=2] {'x'}, dimensions={0}, use_global_device_ids=true | all-gather | bytes 1146880 | tf_op jit(solution)/shard_map/all_gather | solution.py:51
  131.9 4.2 %shard_map.105 = (bf16[128,896]{1,0:T(8,128)(2,1)S(1)}, bf16[128,2048]{1,0:T(8,128)(2,1)S(1)}, bf16[128,2048]{1,0:T(8,128)(2,1)S(1)}) custom-call(bf16[4,128,896]{2,1,0:T(8,128)(2,1)S(1)} %bitcast.52, f32[128,256]{1,0:T(8,128)S(1)} %all_gather.63.refs_1_.refs_6_.refs_3_, bf16[4,256,512]{2,1,0:T(8,128)(2,1)S(1)} %pad.4.refs_2_.refs_7_.refs_4_, ...), custom_call_target="tpu_custom_call" | custom-call | tf_op jit(solution)/shard_map/pallas_call | solution.py:314
  136.1 13.6 %all-gather.3 = bf16[512,896]{1,0:T(8,128)(2,1)S(1)} all-gather(bf16[128,896]{1,0:T(8,128)(2,1)S(1)} %get-tuple-element.29), channel_id=5, replica_groups=mesh['y'=4,'z'=8,'x'=4,'c'=2] {'x'}, dimensions={0}, use_global_device_ids=true | all-gather | bytes 1146880 | tf_op jit(solution)/shard_map/all_gather | solution.py:51
  149.7 4.6 %shard_map.106 = (bf16[128,896]{1,0:T(8,128)(2,1)S(1)}, bf16[128,2048]{1,0:T(8,128)(2,1)S(1)}, bf16[128,2048]{1,0:T(8,128)(2,1)S(1)}) custom-call(bf16[4,128,896]{2,1,0:T(8,128)(2,1)S(1)} %bitcast.55, f32[128,256]{1,0:T(8,128)S(1)} %all_gather.63.refs_1_.refs_6_.refs_3_, bf16[4,256,512]{2,1,0:T(8,128)(2,1)S(1)} %pad.4.refs_2_.refs_7_.refs_4_, ...), custom_call_target="tpu_custom_call" | custom-call | tf_op jit(solution)/shard_map/pallas_call | solution.py:314
  154.3 14.4 %all-gather.4 = bf16[512,896]{1,0:T(8,128)(2,1)S(1)} all-gather(bf16[128,896]{1,0:T(8,128)(2,1)S(1)} %get-tuple-element.31), channel_id=6, replica_groups=mesh['y'=4,'z'=8,'x'=4,'c'=2] {'x'}, dimensions={0}, use_global_device_ids=true | all-gather | bytes 1146880 | tf_op jit(solution)/shard_map/all_gather | solution.py:51
  168.7 4.6 %shard_map.107 = (bf16[128,896]{1,0:T(8,128)(2,1)S(1)}, bf16[128,2048]{1,0:T(8,128)(2,1)S(1)}, bf16[128,2048]{1,0:T(8,128)(2,1)S(1)}) custom-call(bf16[4,128,896]{2,1,0:T(8,128)(2,1)S(1)} %bitcast.58, f32[128,256]{1,0:T(8,128)S(1)} %all_gather.63.refs_1_.refs_6_.refs_3_, bf16[4,256,512]{2,1,0:T(8,128)(2,1)S(1)} %pad.4.refs_2_.refs_7_.refs_4_, ...), custom_call_target="tpu_custom_call" | custom-call | tf_op jit(solution)/shard_map/pallas_call | solution.py:314
  173.3 14.5 %all-gather.5 = bf16[512,896]{1,0:T(8,128)(2,1)} all-gather(bf16[128,896]{1,0:T(8,128)(2,1)S(1)} %get-tuple-element.33), channel_id=7, replica_groups=mesh['y'=4,'z'=8,'x'=4,'c'=2] {'x'}, dimensions={0}, use_global_device_ids=true | all-gather | bytes 1146880 | tf_op jit(solution)/shard_map/all_gather | solution.py:51
  187.8 6.3 %shard_map.108 = (bf16[8,176,128]{2,1,0:T(8,128)(2,1)S(1)}, bf16[8,176,128]{2,1,0:T(8,128)(2,1)S(1)}, bf16[128,512]{1,0:T(8,128)(2,1)S(1)}, bf16[128,2048]{1,0:T(8,128)(2,1)S(1)}) custom-call(s32[2]{0:T(128)S(1)} %pad_add_fusion.refs_0_, bf16[4,128,896]{2,1,0:T(8,128)(2,1)S(1)} %bitcast.53, bf16[4,128,896]{2,1,0:T(8,128)(2,1)} %bitcast.56, ...), custom_call_target="tpu_custom_call" | custom-call | tf_op jit(solution)/shard_map/pallas_call | solution.py:372
  194.1 13.2 %all-gather.6 = bf16[512,512]{1,0:T(8,128)(2,1)S(1)} all-gather(bf16[128,512]{1,0:T(8,128)(2,1)S(1)} %get-tuple-element.36), channel_id=8, replica_groups=mesh['y'=4,'z'=8,'x'=4,'c'=2] {'x'}, dimensions={0}, use_global_device_ids=true | all-gather | bytes 655360 | tf_op jit(solution)/shard_map/all_gather | solution.py:51
  207.4 4.8 %shard_map.109 = (bf16[8,176,128]{2,1,0:T(8,128)(2,1)S(1)}, bf16[8,176,128]{2,1,0:T(8,128)(2,1)S(1)}, bf16[128,512]{1,0:T(8,128)(2,1)S(1)}, bf16[128,2048]{1,0:T(8,128)(2,1)S(1)}) custom-call(s32[2]{0:T(128)S(1)} %pad_add_fusion.refs_0_, bf16[4,128,512]{2,1,0:T(8,128)(2,1)S(1)} %bitcast.66, bf16[4,128,896]{2,1,0:T(8,128)(2,1)} %bitcast.60, ...), custom_call_target="tpu_custom_call" | custom-call | tf_op jit(solution)/shard_map/pallas_call | solution.py:372
  212.3 13.5 %all-gather.7 = bf16[512,512]{1,0:T(8,128)(2,1)S(1)} all-gather(bf16[128,512]{1,0:T(8,128)(2,1)S(1)} %get-tuple-element.39), channel_id=9, replica_groups=mesh['y'=4,'z'=8,'x'=4,'c'=2] {'x'}, dimensions={0}, use_global_device_ids=true | all-gather | bytes 655360 | tf_op jit(solution)/shard_map/all_gather | solution.py:51
  225.8 6.1 %shard_map.110 = (bf16[8,176,128]{2,1,0:T(8,128)(2,1)S(1)}, bf16[8,176,128]{2,1,0:T(8,128)(2,1)S(1)}, bf16[128,512]{1,0:T(8,128)(2,1)S(1)}, bf16[128,2048]{1,0:T(8,128)(2,1)}) custom-call(s32[2]{0:T(128)S(1)} %pad_add_fusion.refs_0_, bf16[4,128,512]{2,1,0:T(8,128)(2,1)S(1)} %bitcast.65, bf16[4,128,896]{2,1,0:T(8,128)(2,1)} %bitcast.57, ...), custom_call_target="tpu_custom_call" | custom-call | tf_op jit(solution)/shard_map/pallas_call | solution.py:372
  231.9 12.9 %all-gather.8 = bf16[512,512]{1,0:T(8,128)(2,1)S(1)} all-gather(bf16[128,512]{1,0:T(8,128)(2,1)S(1)} %get-tuple-element.42), channel_id=10, replica_groups=mesh['y'=4,'z'=8,'x'=4,'c'=2] {'x'}, dimensions={0}, use_global_device_ids=true | all-gather | bytes 655360 | tf_op jit(solution)/shard_map/all_gather | solution.py:51
  244.8 1.7 shard_map.111
  246.6 1.6 collective-permute-done.1
  248.8 22.3 %all_to_all.20 = bf16[4,8,176,128]{3,2,1,0:T(8,128)(2,1)S(1)} all-to-all(bf16[4,8,176,128]{3,2,1,0:T(8,128)(2,1)S(1)} %add_convert_fusion), channel_id=1, replica_groups=mesh['y'=4,'z'=8,'x'=4,'c'=2] {'y'}, dimensions={0} | all-to-all | bytes 2883584 | tf_op jit(solution)/shard_map/all_to_all | solution.py:43
  271.4 17.2 %all_to_all.21 = bf16[8,176,128]{2,1,0:T(8,128)(2,1)S(1)} all-to-all(bf16[8,176,128]{2,1,0:T(8,128)(2,1)S(1)} %reduce_sum.51), channel_id=1, replica_groups=mesh['y'=4,'z'=8,'x'=4,'c'=2] {'z'}, dimensions={0} | all-to-all | bytes 720896 | tf_op jit(solution)/shard_map/all_to_all | solution.py:43
  (66 shorter events, 8.5 us)
Async XLA Ops:
  7.2 106.4 %all-gather.12.cloned.1.call-start = ((), (), s32[]{:S(2)}) async-start(), calls=%async_computation.4 | async-start | bytes 17039360 | tf_op jit(solution)/shard_map/all_gather | solution.py:229
  17.4 4.6 %copy-start.8 = (s32[2,2]{1,0:T(2,128)S(1)}, s32[2,2]{1,0:T(2,128)}, u32[]{:S(2)}) copy-start(s32[2,2]{1,0:T(2,128)} %param.16) | copy-start | bytes 52
  17.4 5.3 %copy-start.7 = (s32[4]{0:T(128)S(1)}, s32[4]{0:T(128)}, u32[]{:S(2)}) copy-start(s32[4]{0:T(128)} %param.17) | copy-start | bytes 52
  17.4 7.7 %copy-start.6 = (f32[1,8192]{1,0:T(1,128)S(1)}, f32[1,8192]{1,0:T(1,128)}, u32[]{:S(2)}) copy-start(f32[1,8192]{1,0:T(1,128)} %param.15) | copy-start | bytes 98308
  17.5 8.5 %copy-start.5 = (bf16[1,160,512]{2,1,0:T(8,128)(2,1)S(1)}, bf16[1,160,512]{2,1,0:T(8,128)(2,1)}, u32[]{:S(2)}) copy-start(bf16[1,160,512]{2,1,0:T(8,128)(2,1)} %param.14) | copy-start | bytes 491524
  17.5 41.1 %all-to-all-start.1 = ((bf16[4,80,2048]{2,1,0:T(8,128)(2,1)}), bf16[4,80,2048]{2,1,0:T(8,128)(2,1)}, u32[]{:S(2)}, u32[]{:S(2)}) async-start(bf16[4,80,2048]{2,1,0:T(8,128)(2,1)} %broadcast_in_dim.52), calls=%async_computation.1 | async-start | bytes 2621440 | tf_op jit(solution)/shard_map/all_to_all | solution.py:43
  53.6 1.5 copy-start.4
  56.8 1.3 slice-start
  58.2 110.4 %copy-start = (bf16[4,256,512]{2,1,0:T(8,128)(2,1)}, bf16[4,256,512]{2,1,0:T(8,128)(2,1)S(1)}, u32[]{:S(2)}) copy-start(bf16[4,256,512]{2,1,0:T(8,128)(2,1)S(1)} %pad.4.refs_2_.refs_7_.refs_4_) | copy-start | bytes 3145732
  58.6 21.1 %all-to-all-start = ((bf16[4,2,32,2048]{3,2,1,0:T(8,128)(2,1)}), bf16[4,2,32,2048]{3,2,1,0:T(8,128)(2,1)S(1)}, u32[]{:S(2)}, u32[]{:S(2)}) async-start(bf16[4,2,32,2048]{3,2,1,0:T(8,128)(2,1)} %reshape.89), calls=%async_computation | async-start | bytes 2097152 | tf_op jit(solution)/shard_map/all_to_all | solution.py:43
  63.4 16.4 %collective-permute-start = (bf16[4,80,2048]{2,1,0:T(8,128)(2,1)}, bf16[4,80,2048]{2,1,0:T(8,128)(2,1)}, u32[]{:S(2)}, u32[]{:S(2)}) collective-permute-start(bf16[4,80,2048]{2,1,0:T(8,128)(2,1)} %all-to-all-done.1), channel_id=1, source_target_pairs={{0,1},{1,0},{2,3},{3,2},{4,5},{5,4},{6,7},{7,6},{8,9},{9,8},{10,11... | collective-permute-start | bytes 3932168 | tf_op jit(solution)/shard_map/ppermute | solution.py:255
  149.7 4.6 %copy-start.2 = (bf16[512,896]{1,0:T(8,128)(2,1)}, bf16[512,896]{1,0:T(8,128)(2,1)S(1)}, u32[]{:S(2)}) copy-start(bf16[512,896]{1,0:T(8,128)(2,1)S(1)} %all-gather.3) | copy-start | bytes 2752516
  168.7 4.6 %copy-start.3 = (bf16[512,896]{1,0:T(8,128)(2,1)}, bf16[512,896]{1,0:T(8,128)(2,1)S(1)}, u32[]{:S(2)}) copy-start(bf16[512,896]{1,0:T(8,128)(2,1)S(1)} %all-gather.4) | copy-start | bytes 2752516
  194.0 52.6 %collective-permute-start.4 = (bf16[8,176,128]{2,1,0:T(8,128)(2,1)S(1)}, bf16[8,176,128]{2,1,0:T(8,128)(2,1)S(1)}, u32[]{:S(2)}, u32[]{:S(2)}) collective-permute-start(bf16[8,176,128]{2,1,0:T(8,128)(2,1)S(1)} %get-tuple-element.51), channel_id=1, source_target_pairs={{0,1},{1,0},{2,3},{3,2},{4,5},{5,4},{6,7},{7,6},{8,9},{9,8},{10,11... | collective-permute-start | bytes 1081352 | tf_op jit(solution)/shard_map/ppermute | solution.py:382
  212.2 34.4 %collective-permute-start.3 = (bf16[8,176,128]{2,1,0:T(8,128)(2,1)S(1)}, bf16[8,176,128]{2,1,0:T(8,128)(2,1)S(1)}, u32[]{:S(2)}, u32[]{:S(2)}) collective-permute-start(bf16[8,176,128]{2,1,0:T(8,128)(2,1)S(1)} %get-tuple-element.50), channel_id=1, source_target_pairs={{0,1},{1,0},{2,3},{3,2},{4,5},{5,4},{6,7},{7,6},{8,9},{9,8},{10,11... | collective-permute-start | bytes 1081352 | tf_op jit(solution)/shard_map/ppermute | solution.py:382
  225.8 19.0 %copy-start.1 = (bf16[4,256,512]{2,1,0:T(8,128)(2,1)S(1)}, bf16[4,256,512]{2,1,0:T(8,128)(2,1)}, u32[]{:S(2)}) copy-start(bf16[4,256,512]{2,1,0:T(8,128)(2,1)} %copy-done) | copy-start | bytes 3145732
  231.9 14.7 %collective-permute-start.2 = (bf16[8,176,128]{2,1,0:T(8,128)(2,1)S(1)}, bf16[8,176,128]{2,1,0:T(8,128)(2,1)S(1)}, u32[]{:S(2)}, u32[]{:S(2)}) collective-permute-start(bf16[8,176,128]{2,1,0:T(8,128)(2,1)S(1)} %get-tuple-element.49), channel_id=1, source_target_pairs={{0,1},{1,0},{2,3},{3,2},{4,5},{5,4},{6,7},{7,6},{8,9},{9,8},{10,11... | collective-permute-start | bytes 1081352 | tf_op jit(solution)/shard_map/ppermute | solution.py:382
  246.5 1.8 collective-permute-start.1
Sparse Core Ops, SparseCore 0:
  10.7 102.8 all-gather.11

commit v4 on v3

--- a/solution.py
+++ b/solution.py
@@ -17,6 +17,7 @@
 LANES = 128
 STEP = 1024
 INTERPRET = False
+REST = 128
 KERNEL_BYTES = 50 * 1024 * 1024
 
 
@@ -26,7 +27,7 @@
     )
 
 
-def coefficient_row(adapter, adapter_rank_blocks, packed, columns):
+def coefficient_table(adapter_rank_blocks, packed, columns):
     rank_sizes = 8 * adapter_rank_blocks
     adapters = jnp.arange(ADAPTERS, dtype=jnp.int32)
     ends = jnp.sum(
@@ -34,9 +35,13 @@
     )
     column = jnp.arange(columns, dtype=jnp.int32)
     owner = jnp.sum((column[:, None] >= ends[None, :]).astype(jnp.int32), axis=1)
-    rank = jnp.sum(jnp.where(adapters == adapter, rank_sizes, 0)).astype(F32)
-    held = (owner == adapter) & (column < packed)
-    return jnp.where(held, ADAPTER_ALPHA / rank, 0.0)[None, :]
+    owner = jnp.where(column < packed, owner, -1)
+    rank = jnp.sum(
+        jnp.where(owner[:, None] == adapters[None, :], rank_sizes[None, :], 0), axis=1
+    ).astype(F32)
+    value = jnp.where(owner >= 0, ADAPTER_ALPHA / jnp.maximum(rank, 1.0), 0.0)
+    spare = jnp.zeros((6, columns), F32)
+    return jnp.concatenate([owner.astype(F32)[None], value[None], spare], axis=0)
 
 
 def exchanged(value, axis):
@@ -51,23 +56,25 @@
     return lax.all_gather(partial, "x", axis=0, tiled=False)
 
 
-def token_stats(gathered_ref, value_cols, chunk, packed, width):
+def token_stats(gathered_ref, table, value_cols, chunk, packed, width):
     total = gathered_ref[...].astype(F32).sum(axis=0)
     side = total[:, value_cols + chunk :]
     mean = (side[:, packed : packed + 1] + side[:, packed + 1 : packed + 2]) / width
-    return total[:, :value_cols], side, lax.rsqrt(mean + EPSILON)
+    adapter = side[:, packed + 2 : packed + 3]
+    coef = jnp.where(table[:1, :] == adapter, table[1:2, :], 0.0)
+    return total[:, :value_cols], side, lax.rsqrt(mean + EPSILON), coef
 
 
 def forward_kernel(*refs, layer, sizes):
     value_cols, chunk, packed, width = sizes
     first = layer == 0
     if first:
-        grad, last_out, state, value_w, down_w, gain, sent, last_sum, scaled = refs[:9]
-        acc, side_acc, square_acc, last_acc = refs[9:]
+        own_ids, grad, last_out, last_rest, state, value_w, down_w, gain = refs[:8]
+        sent, last_sum, scaled, acc, side_acc, square_acc, last_acc = refs[8:]
     else:
-        before, coef, up, state, out_w, value_w, down_w, gain, last_piece = refs[:9]
-        sent, new_state, scaled = refs[9:12]
-        acc, side_acc, square_acc, values = refs[12:]
+        own_ids, before, table, up, state, out_w, rest_w, value_w, down_w, gain = refs[:10]
+        last_piece, sent, new_state, scaled = refs[10:14]
+        acc, side_acc, square_acc, values = refs[14:]
     step = pl.program_id(0)
 
     @pl.when(step == 0)
@@ -78,15 +85,21 @@
         if first:
             last_acc[...] = jnp.zeros_like(last_acc)
         else:
-            value_part, side, inv = token_stats(before, value_cols, chunk, packed, width)
-            low = (side * inv * coef[...]).astype(BF)
+            value_part, side, inv, coef = token_stats(
+                before, table, value_cols, chunk, packed, width
+            )
+            low = (side * inv * coef).astype(BF)
             values[...] = (value_part * inv + contract(low, up[layer - 1], 1, 0)).astype(BF)
 
     if first:
         wide = state[...].astype(F32)
-        last_acc[...] += contract(grad[...], last_out[0], 1, 0)
+        most = last_out.shape[2]
+        last_acc[:, :most] += contract(grad[...], last_out[0], 1, 0)
+        last_acc[:, most:] += contract(grad[...], last_rest[0], 1, 1)
     else:
-        wide = state[...].astype(F32) + contract(values[...], out_w[0], 1, 1)
+        most = out_w.shape[2]
+        wide = state[...].astype(F32) + contract(values[:, :most], out_w[0], 1, 1)
+        wide = wide + contract(values[:, most:], rest_w[0], 1, 0)
         new_state[...] = wide.astype(BF)
         wide = new_state[...].astype(F32)
     square_acc[...] += jnp.sum(wide * wide, axis=1, keepdims=True)
@@ -111,6 +124,7 @@
         lane = lax.broadcasted_iota(jnp.int32, side_acc.shape, 1)
         side = jnp.where(lane == packed, high, side_acc[...])
         side = jnp.where(lane == packed + 1, squares - high, side)
+        side = jnp.where(lane == packed + 2, own_ids[:, :1], side)
         sent[:, value_cols + chunk :] = side.astype(BF)
 
 
@@ -122,9 +136,9 @@
     take = lambda n: [refs.pop(0) for _ in range(n)]
     where, = take(1)
     pieces = take(value_cols // chunk if last else 1)
-    before, coef, up, scaled = take(4)
+    before, table, up, scaled = take(4)
     if not bottom:
-        state, grad, value_w, down_w, gain, out_w = take(6)
+        state, grad, value_w, down_w, gain, out_w, rest_w = take(7)
     own, other = take(2)
     if not bottom:
         sent, new_grad = take(2)
@@ -144,9 +158,11 @@
         total = summed_pieces[0] if len(pieces) == 1 else jnp.concatenate(summed_pieces, axis=1)
         value_grad = total.astype(BF)
         wide_value = value_grad.astype(F32)
-        low_grad = (contract(value_grad, up[layer], 1, 1) * coef[...]).astype(BF)
+        value_part, side, inv, coef = token_stats(
+            before, table, value_cols, chunk, packed, width
+        )
+        low_grad = (contract(value_grad, up[layer], 1, 1) * coef).astype(BF)
         wide_low = low_grad.astype(F32)
-        value_part, side, inv = token_stats(before, value_cols, chunk, packed, width)
         mixed_low[...] = (wide_low * inv).astype(BF)
         if not bottom:
             mixed_value[...] = (wide_value * inv).astype(BF)
@@ -154,7 +170,7 @@
             inner = inner + jnp.sum(side * wide_low, axis=1, keepdims=True)
             kappa[...] = jnp.broadcast_to(inv * inv * inv * inner / width, kappa.shape)
             acc[...] = jnp.zeros_like(acc)
-        low = (side * inv * coef[...]).astype(BF)
+        low = (side * inv * coef).astype(BF)
         raised[...] = contract(value_grad, low, 0, 0)
         for z in range(nz):
             for target, core in ((own, ci), (other, 1 - ci)):
@@ -179,7 +195,9 @@
         wide = grad[...].astype(F32) + gain[0] * back - kappa[:, :1] * state[...].astype(F32)
         updated = wide.astype(BF)
         new_grad[...] = updated
-        acc[...] += contract(updated, out_w[0], 1, 0)
+        most = out_w.shape[2]
+        acc[:, :most] += contract(updated, out_w[0], 1, 0)
+        acc[:, most:] += contract(updated, rest_w[0], 1, 1)
 
         @pl.when(step == pl.num_programs(0) - 1)
         def _():
@@ -194,8 +212,18 @@
     return pl.BlockSpec((tokens, STEP), lambda i: (0, i))
 
 
-def weight(layer, half, cols):
-    return pl.BlockSpec((1, STEP, cols), lambda i: (layer, i, half))
+def value_part_of(layer, cols):
+    return pl.BlockSpec((1, STEP, cols), lambda i: (layer, i, 0))
+
+
+def out_parts_of(layer, cols):
+    return [
+        pl.BlockSpec(
+            (pl.Element(1), pl.Element(STEP), pl.Element(cols - REST)),
+            lambda i: (layer, i * STEP, cols),
+        ),
+        pl.BlockSpec((1, REST, STEP), lambda i: (layer, 0, i)),
+    ]
 
 
 def along(layer, rows):
@@ -224,11 +252,13 @@
     lanes = nc * rows
     depth = nz * lanes
 
-    joined = jnp.concatenate([value_projection_weight[0], output_weight[0].T], axis=1)
+    most = value_cols - REST
+    joined = jnp.concatenate([value_projection_weight[0], output_weight[0, :most].T], axis=1)
     joined = with_layout_constraint(joined, Layout(major_to_minor=(0, 1)))
     full = lax.all_gather(joined, GROUP, axis=0, tiled=False)
     full = with_layout_constraint(full, Layout(major_to_minor=(0, 1, 2)))
-    full = full.reshape(layers, depth, 2 * value_cols)
+    full = full.reshape(layers, depth, value_cols + most)
+    rest = lax.all_gather(output_weight[0, most:], "z", axis=0, tiled=False)
 
     all_tokens = residual_input.shape[0] * residual_input.shape[1]
     tokens = all_tokens // ny
@@ -245,17 +275,20 @@
     grad = spread[:, 1].reshape(nx * tokens, depth)
 
     padded = -(-packed // LANES) * LANES
-    half = packed // nc
     down_half = lax.dynamic_slice(
-        adapter_down_weight[0].T.reshape(packed, nz, nx, lanes),
-        (ci * half, 0, xi, 0),
-        (half, nz, 1, lanes),
-    ).reshape(1, half, depth)
-    mine = exchanged(jnp.broadcast_to(down_half, (layers, half, depth)), "y")
+        adapter_down_weight[0].T.reshape(packed, nz, nx, nc, rows),
+        (0, 0, xi, ci, 0),
+        (packed, nz, 1, 1, rows),
+    ).reshape(packed, nz * rows)
+    rest = rest.transpose(1, 0, 2).reshape(REST, nz * rows)
+    beside = jnp.concatenate([down_half, rest], axis=0)
+    mine = exchanged(jnp.broadcast_to(beside[None], (layers,) + beside.shape), "y")
     theirs = lax.ppermute(mine, "c", [(j, 1 - j) for j in range(nc)])
     ordered = [jnp.where(ci == 0, mine, theirs), jnp.where(ci == 0, theirs, mine)]
-    filler = jnp.zeros((layers, padded - packed, depth), BF)
-    downs_full = jnp.concatenate(ordered + [filler], axis=1)
+    pieces = [part[..., z * rows : (z + 1) * rows] for z in range(nz) for part in ordered]
+    downs_full = jnp.concatenate([piece[:, :packed] for piece in pieces], axis=2)
+    downs_full = jnp.pad(downs_full, ((0, 0), (0, padded - packed), (0, 0)))
+    rest_full = jnp.concatenate([piece[:, packed:] for piece in pieces], axis=2)
 
     gain_own = lax.dynamic_index_in_dim(
         input_norm_scale.reshape(nz, nx, lanes), xi, 1, keepdims=False
@@ -269,10 +302,10 @@
     gains = small[:, packed:].astype(F32).reshape(layers, 3, 1, depth)
     gains = gains[:, 0] + gains[:, 1] + gains[:, 2]
     adapter = lax.dynamic_index_in_dim(segment_adapter_index.reshape(ny), yi, 0, keepdims=False)
-    coef_row = coefficient_row(adapter, adapter_rank_blocks, packed, padded)
-    coef = lax.all_gather(
-        jnp.broadcast_to(coef_row, (tokens, padded)), "x", axis=0, tiled=True
-    )
+    table = coefficient_table(adapter_rank_blocks, packed, padded)
+    holder = jnp.arange(nx * tokens, dtype=jnp.int32)[:, None] // tokens
+    own_ids = jnp.where(holder == xi, adapter.astype(F32), 0.0)
+    own_ids = jnp.broadcast_to(own_ids, (nx * tokens, LANES))
 
     count = nx * tokens
     chunk = value_cols // layers
@@ -299,16 +332,17 @@
         functools.partial(forward_kernel, layer=0, sizes=sizes),
         out_shape=(sent_shape, shape((count, value_cols), BF), wide_shape),
         in_specs=[
+            whole(),
             columns(count),
-            weight(top, 1, value_cols),
+            *out_parts_of(top, value_cols),
             columns(count),
-            weight(0, 0, value_cols),
+            value_part_of(0, value_cols),
             along(0, padded),
             along(0, 1),
         ],
         out_specs=(whole(), whole(), columns(count)),
         scratch_shapes=sums + [pltpu.VMEM((count, value_cols), F32)],
-    )(grad, full, state, full, downs_full, gains)
+    )(own_ids, grad, full, rest_full, state, full, downs_full, gains)
     arrived, inputs, scaled = [gathered(sent)], [state], [scaled_input]
     for layer in range(1, layers):
         sent, state, scaled_input = call(
@@ -318,16 +352,29 @@
                 whole(),
                 whole(),
                 whole(),
+                whole(),
                 columns(count),
-                weight(layer - 1, 1, value_cols),
-                weight(layer, 0, value_cols),
+                *out_parts_of(layer - 1, value_cols),
+                value_part_of(layer, value_cols),
                 along(layer, padded),
                 along(layer, 1),
                 whole(),
             ],
             out_specs=(whole(), columns(count), columns(count)),
             scratch_shapes=sums + [pltpu.VMEM((count, value_cols), BF)],
-        )(arrived[-1], coef, ups, state, full, full, downs_full, gains, last)
+        )(
+            own_ids,
+            arrived[-1],
+            table,
+            ups,
+            state,
+            full,
+            rest_full,
+            full,
+            downs_full,
+            gains,
+            last,
+        )
         arrived.append(gathered(sent))
         inputs.append(state)
         scaled.append(scaled_input)
@@ -340,7 +387,7 @@
     pieces = arrived
     for layer in reversed(range(layers)):
         bottom = layer == 0
-        operands = [place_ids, *pieces, arrived[layer], coef, ups, scaled[layer]]
+        operands = [place_ids, *pieces, arrived[layer], table, ups, scaled[layer]]
         specs = [
             pl.BlockSpec(memory_space=pltpu.SMEM),
             *[whole() for _ in pieces],
@@ -353,14 +400,14 @@
         out_specs = [whole()] * 2
         scratch = [pltpu.VMEM((count, padded), BF), pltpu.VMEM((value_cols, padded), F32)]
         if not bottom:
-            operands += [inputs[layer], grad, full, downs_full, gains, full]
+            operands += [inputs[layer], grad, full, downs_full, gains, full, rest_full]
             specs += [
                 columns(count),
                 columns(count),
-                weight(layer, 0, value_cols),
+                value_part_of(layer, value_cols),
                 along(layer, padded),
                 along(layer, 1),
-                weight(layer - 1, 1, value_cols),
+                *out_parts_of(layer - 1, value_cols),
             ]
             outs += [shape((count, value_cols), BF), wide_shape]
             out_specs += [whole(), columns(count)]

time: 297 us -> 321 us (1.081)
  blocking collectives: 180 us -> 214 us
  waiting for transfers between devices: 30.3 us -> 10.8 us
  local copies, waits for them, and re-layouts: 14.5 us -> 24.1 us
  other arithmetic: 12 us -> 7.86 us
    all_gather x1, waiting for transfers between devices: 28.6 us -> 0.02 us  [local(): full = lax.all_gather(joined, GROUP, axis=0, tiled=False)]
    all_gather x1, blocking collectives: 27.6 us -> 50.1 us  [local(): small = lax.all_gather(small, 'y', axis=0, tiled=False)]
    all_gather x1, blocking collectives: 15.5 us -> 28.5 us  [local(): rest = lax.all_gather(output_weight[0, most:], 'z', axis=0, tiled=False)]
    all_to_all x2, waiting for transfers between devices: 0.01 us -> 9.09 us  [exchanged(): return lax.all_to_all(value, axis, split_axis=0, concat_axis=0, tiled=True)]
    unnamed x21 -> x61, local copies, waits for them, and re-layouts: 1.63 us -> 5.32 us
  transfers between devices with their start and end apart: 8 -> 8, of which waited for: 2 -> 2; matrix products, arithmetic and copies ran while one was open for 7% -> 8% of each run, Pallas kernels for 4% -> 4%
where the time goes in v4:
time: 321 us; the launch traced here: 318 us
  blocking collectives  214 us (67%)
  Pallas kernels  36.6 us (11%)
  local copies, waits for them, and re-layouts  24.1 us (8%)
  between operations  15.3 us (5%)
  waiting for transfers between devices  10.8 us (3%)
  starting transfers between devices  9.81 us (3%)
  other arithmetic  7.86 us (2%)
    all_gather x7, blocking collectives, gathered(): return lax.all_gather(partial, 'x', axis=0, tiled=False)  96.7 us
    all_gather x1, blocking collectives, local(): small = lax.all_gather(small, 'y', axis=0, tiled=False)  50.1 us
    all_to_all x2, blocking collectives, exchanged(): return lax.all_to_all(value, axis, split_axis=0, concat_axis=0, tiled=True)  38.3 us
    all_gather x1, blocking collectives, local(): rest = lax.all_gather(output_weight[0, most:], 'z', axis=0, tiled=False)  28.5 us
    pallas_call x4, Pallas kernels, local(): call(functools.partial(backward_kernel, layer=layer, last=layer == top, s...  19.6 us
    pallas_call x3, Pallas kernels, local(): call(functools.partial(forward_kernel, layer=layer, sizes=sizes), out_sha...  13.7 us
    all_to_all x2, starting transfers between devices, exchanged(): return lax.all_to_all(value, axis, split_axis=0, concat_axis=0, tiled=True)  9.49 us
    all_to_all x2, waiting for transfers between devices, exchanged(): return lax.all_to_all(value, axis, split_axis=0, concat_axis=0, tiled=True)  9.09 us
  transfers between devices with their start and end apart: 8, of which 2 were waited for; matrix products, arithmetic and copies ran while one was open for 8% of the time, Pallas kernels for 4%

profile of v4, /device:TPU:2, one launch (start us, length us, event | category | flops | bytes accessed | tf_op | source)
XLA Modules:
  0.0 318.2 jit_solution(15416673265696848560)
XLA Ops:
  8.2 1.6 pad_maximum_fusion.1
  10.7 28.5 %all_gather.59 = bf16[8,128,128]{2,1,0:T(8,128)(2,1)S(1)} all-gather(bf16[1,128,128]{2,1,0:T(8,128)(2,1)S(1)} %slice.185), channel_id=1, replica_groups=mesh['y'=4,'z'=8,'x'=4,'c'=2] {'z'}, dimensions={0}, use_global_device_ids=true | all-gather | bytes 294912 | tf_op jit(solution)/shard_map/all_gather | solution.py:261
  39.5 4.2 %reshape.183 = bf16[160,8,4,2,128]{4,3,2,1,0:T(2,128)(2,1)S(1)} reshape(bf16[160,8192]{1,0:T(8,128)(2,1)} %bitcast.95) | data formatting | bytes 5242880 | tf_op jit(solution)/shard_map/reshape | solution.py:279
  43.8 1.9 dynamic-slice_reduce_fusion
  45.8 1.7 broadcast_in_dim.76
  47.5 4.7 %all-to-all-start.1 = ((bf16[4,288,1024]{2,1,0:T(8,128)(2,1)}), bf16[4,288,1024]{2,1,0:T(8,128)(2,1)}, u32[]{:S(2)}, u32[]{:S(2)}) async-start(bf16[4,288,1024]{2,1,0:T(8,128)(2,1)} %broadcast_in_dim.76), calls=%async_computation.1 | async-start | bytes 4718592 | tf_op jit(solution)/shard_map/all_to_all | solution.py:48
  53.6 50.1 %all-gather.9 = bf16[4,172,512]{2,1,0:T(8,128)(2,1)S(1)} all-gather(bf16[1,172,512]{2,1,0:T(8,128)(2,1)S(1)} %maximum_bitcast_fusion.1), channel_id=3, replica_groups=mesh['y'=4,'z'=8,'x'=4,'c'=2] {'y'}, dimensions={0}, use_global_device_ids=true | all-gather | bytes 880640 | tf_op jit(solution)/shard_map/all_gather | solution.py:300
  105.1 1.3 constant_dynamic-slice_fusion
  108.1 1.3 reshape.181
  109.8 4.8 %all-to-all-start = ((bf16[4,2,32,2048]{3,2,1,0:T(8,128)(2,1)}), bf16[4,2,32,2048]{3,2,1,0:T(8,128)(2,1)S(1)}, u32[]{:S(2)}, u32[]{:S(2)}) async-start(bf16[4,2,32,2048]{3,2,1,0:T(8,128)(2,1)} %reshape.181), calls=%async_computation | async-start | bytes 2097152 | tf_op jit(solution)/shard_map/all_to_all | solution.py:48
  115.0 9.1 %all-to-all-done = bf16[4,2,32,2048]{3,2,1,0:T(8,128)(2,1)S(1)} async-done(((bf16[4,2,32,2048]{3,2,1,0:T(8,128)(2,1)}), bf16[4,2,32,2048]{3,2,1,0:T(8,128)(2,1)S(1)}, u32[]{:S(2)}, u32[]{:S(2)}) %all-to-all-start) | async-done | bytes 1048608 | tf_op jit(solution)/shard_map/all_to_all | solution.py:48
  125.2 2.7 broadcast_select_fusion
  129.3 2.4 pad.8.refs_6_.refs_8_.refs_12_.refs_9_
  132.9 1.4 copy-done.5
  135.4 3.3 %shard_map.104 = (bf16[128,896]{1,0:T(8,128)(2,1)S(1)}, bf16[128,512]{1,0:T(8,128)(2,1)S(1)}, bf16[128,2048]{1,0:T(8,128)(2,1)S(1)}) custom-call(f32[128,128]{1,0:T(8,128)S(1)} %broadcast_in_dim.75.refs_0_, bf16[128,2048]{1,0:T(8,128)(2,1)S(1)} %bitcast.68, bf16[4,2048,896]{2,1,0:T(8,128)(2,1)} %bitcast.79, ...), custom_call_target="tpu_custom_call" | custom-call | tf_op jit(solution)/shard_map/pallas_call | solution.py:331
  138.7 13.0 %all-gather.2 = bf16[512,896]{1,0:T(8,128)(2,1)S(1)} all-gather(bf16[128,896]{1,0:T(8,128)(2,1)S(1)} %get-tuple-element.27), channel_id=4, replica_groups=mesh['y'=4,'z'=8,'x'=4,'c'=2] {'x'}, dimensions={0}, use_global_device_ids=true | all-gather | bytes 1146880 | tf_op jit(solution)/shard_map/all_gather | solution.py:56
  151.7 4.4 %shard_map.105 = (bf16[128,896]{1,0:T(8,128)(2,1)S(1)}, bf16[128,2048]{1,0:T(8,128)(2,1)S(1)}, bf16[128,2048]{1,0:T(8,128)(2,1)S(1)}) custom-call(f32[128,128]{1,0:T(8,128)S(1)} %broadcast_in_dim.75.refs_0_, bf16[4,128,896]{2,1,0:T(8,128)(2,1)S(1)} %bitcast.59, f32[8,256]{1,0:T(8,128)S(1)} %maximum_maximum_fusion.refs_2_.refs_6_.refs_3_, ...), custom_call_target="tpu_custom_call" | custom-call | tf_op jit(solution)/shard_map/pallas_call | solution.py:348
  156.0 13.9 %all-gather.3 = bf16[512,896]{1,0:T(8,128)(2,1)S(1)} all-gather(bf16[128,896]{1,0:T(8,128)(2,1)S(1)} %get-tuple-element.29), channel_id=5, replica_groups=mesh['y'=4,'z'=8,'x'=4,'c'=2] {'x'}, dimensions={0}, use_global_device_ids=true | all-gather | bytes 1146880 | tf_op jit(solution)/shard_map/all_gather | solution.py:56
  169.9 4.7 %shard_map.106 = (bf16[128,896]{1,0:T(8,128)(2,1)S(1)}, bf16[128,2048]{1,0:T(8,128)(2,1)S(1)}, bf16[128,2048]{1,0:T(8,128)(2,1)S(1)}) custom-call(f32[128,128]{1,0:T(8,128)S(1)} %broadcast_in_dim.75.refs_0_, bf16[4,128,896]{2,1,0:T(8,128)(2,1)S(1)} %bitcast.62, f32[8,256]{1,0:T(8,128)S(1)} %maximum_maximum_fusion.refs_2_.refs_6_.refs_3_, ...), custom_call_target="tpu_custom_call" | custom-call | tf_op jit(solution)/shard_map/pallas_call | solution.py:348
  174.6 14.8 %all-gather.4 = bf16[512,896]{1,0:T(8,128)(2,1)S(1)} all-gather(bf16[128,896]{1,0:T(8,128)(2,1)S(1)} %get-tuple-element.31), channel_id=6, replica_groups=mesh['y'=4,'z'=8,'x'=4,'c'=2] {'x'}, dimensions={0}, use_global_device_ids=true | all-gather | bytes 1146880 | tf_op jit(solution)/shard_map/all_gather | solution.py:56
  189.4 4.7 %shard_map.107 = (bf16[128,896]{1,0:T(8,128)(2,1)S(1)}, bf16[128,2048]{1,0:T(8,128)(2,1)S(1)}, bf16[128,2048]{1,0:T(8,128)(2,1)S(1)}) custom-call(f32[128,128]{1,0:T(8,128)S(1)} %broadcast_in_dim.75.refs_0_, bf16[4,128,896]{2,1,0:T(8,128)(2,1)S(1)} %bitcast.65, f32[8,256]{1,0:T(8,128)S(1)} %maximum_maximum_fusion.refs_2_.refs_6_.refs_3_, ...), custom_call_target="tpu_custom_call" | custom-call | tf_op jit(solution)/shard_map/pallas_call | solution.py:348
  194.1 14.8 %all-gather.5 = bf16[512,896]{1,0:T(8,128)(2,1)} all-gather(bf16[128,896]{1,0:T(8,128)(2,1)S(1)} %get-tuple-element.33), channel_id=7, replica_groups=mesh['y'=4,'z'=8,'x'=4,'c'=2] {'x'}, dimensions={0}, use_global_device_ids=true | all-gather | bytes 1146880 | tf_op jit(solution)/shard_map/all_gather | solution.py:56
  208.9 6.5 %shard_map.108 = (bf16[8,176,128]{2,1,0:T(8,128)(2,1)S(1)}, bf16[8,176,128]{2,1,0:T(8,128)(2,1)S(1)}, bf16[128,512]{1,0:T(8,128)(2,1)S(1)}, bf16[128,2048]{1,0:T(8,128)(2,1)S(1)}) custom-call(s32[2]{0:T(128)S(1)} %pad_add_fusion.refs_0_, bf16[4,128,896]{2,1,0:T(8,128)(2,1)S(1)} %bitcast.60, bf16[4,128,896]{2,1,0:T(8,128)(2,1)} %bitcast.63, ...), custom_call_target="tpu_custom_call" | custom-call | tf_op jit(solution)/shard_map/pallas_call | solution.py:419
  215.6 13.3 %all-gather.6 = bf16[512,512]{1,0:T(8,128)(2,1)S(1)} all-gather(bf16[128,512]{1,0:T(8,128)(2,1)S(1)} %get-tuple-element.36), channel_id=8, replica_groups=mesh['y'=4,'z'=8,'x'=4,'c'=2] {'x'}, dimensions={0}, use_global_device_ids=true | all-gather | bytes 655360 | tf_op jit(solution)/shard_map/all_gather | solution.py:56
  228.9 5.0 %shard_map.109 = (bf16[8,176,128]{2,1,0:T(8,128)(2,1)S(1)}, bf16[8,176,128]{2,1,0:T(8,128)(2,1)S(1)}, bf16[128,512]{1,0:T(8,128)(2,1)S(1)}, bf16[128,2048]{1,0:T(8,128)(2,1)S(1)}) custom-call(s32[2]{0:T(128)S(1)} %pad_add_fusion.refs_0_, bf16[4,128,512]{2,1,0:T(8,128)(2,1)S(1)} %bitcast.73, bf16[4,128,896]{2,1,0:T(8,128)(2,1)} %bitcast.67, ...), custom_call_target="tpu_custom_call" | custom-call | tf_op jit(solution)/shard_map/pallas_call | solution.py:419
  234.0 13.5 %all-gather.7 = bf16[512,512]{1,0:T(8,128)(2,1)S(1)} all-gather(bf16[128,512]{1,0:T(8,128)(2,1)S(1)} %get-tuple-element.39), channel_id=9, replica_groups=mesh['y'=4,'z'=8,'x'=4,'c'=2] {'x'}, dimensions={0}, use_global_device_ids=true | all-gather | bytes 655360 | tf_op jit(solution)/shard_map/all_gather | solution.py:56
  247.5 6.4 %shard_map.110 = (bf16[8,176,128]{2,1,0:T(8,128)(2,1)S(1)}, bf16[8,176,128]{2,1,0:T(8,128)(2,1)S(1)}, bf16[128,512]{1,0:T(8,128)(2,1)S(1)}, bf16[128,2048]{1,0:T(8,128)(2,1)}) custom-call(s32[2]{0:T(128)S(1)} %pad_add_fusion.refs_0_, bf16[4,128,512]{2,1,0:T(8,128)(2,1)S(1)} %bitcast.72, bf16[4,128,896]{2,1,0:T(8,128)(2,1)} %bitcast.64, ...), custom_call_target="tpu_custom_call" | custom-call | tf_op jit(solution)/shard_map/pallas_call | solution.py:419
  253.9 13.5 %all-gather.8 = bf16[512,512]{1,0:T(8,128)(2,1)S(1)} all-gather(bf16[128,512]{1,0:T(8,128)(2,1)S(1)} %get-tuple-element.42), channel_id=10, replica_groups=mesh['y'=4,'z'=8,'x'=4,'c'=2] {'x'}, dimensions={0}, use_global_device_ids=true | all-gather | bytes 655360 | tf_op jit(solution)/shard_map/all_gather | solution.py:56
  267.4 1.7 shard_map.111
  269.2 1.6 collective-permute-done.1
  271.4 22.8 %all_to_all.20 = bf16[4,8,176,128]{3,2,1,0:T(8,128)(2,1)S(1)} all-to-all(bf16[4,8,176,128]{3,2,1,0:T(8,128)(2,1)S(1)} %add_convert_fusion), channel_id=1, replica_groups=mesh['y'=4,'z'=8,'x'=4,'c'=2] {'y'}, dimensions={0} | all-to-all | bytes 2883584 | tf_op jit(solution)/shard_map/all_to_all | solution.py:48
  294.5 15.5 %all_to_all.21 = bf16[8,176,128]{2,1,0:T(8,128)(2,1)S(1)} all-to-all(bf16[8,176,128]{2,1,0:T(8,128)(2,1)S(1)} %reduce_sum.54), channel_id=1, replica_groups=mesh['y'=4,'z'=8,'x'=4,'c'=2] {'z'}, dimensions={0} | all-to-all | bytes 720896 | tf_op jit(solution)/shard_map/all_to_all | solution.py:48
  (119 shorter events, 13.7 us)
Async XLA Ops:
  7.2 125.7 %all-gather.12.cloned.1.call-start = ((), (), s32[]{:S(2)}) async-start(), calls=%async_computation.4 | async-start | bytes 14909440 | tf_op jit(solution)/shard_map/all_gather | solution.py:258
  47.5 5.2 %copy-start.11 = (f32[1,8192]{1,0:T(1,128)S(1)}, f32[1,8192]{1,0:T(1,128)}, u32[]{:S(2)}) copy-start(f32[1,8192]{1,0:T(1,128)} %param.15) | copy-start | bytes 98308
  47.5 6.0 %copy-start.10 = (bf16[1,160,512]{2,1,0:T(8,128)(2,1)S(1)}, bf16[1,160,512]{2,1,0:T(8,128)(2,1)}, u32[]{:S(2)}) copy-start(bf16[1,160,512]{2,1,0:T(8,128)(2,1)} %param.14) | copy-start | bytes 491524
  47.5 56.2 %copy-start.12 = (s32[2,2]{1,0:T(2,128)S(1)}, s32[2,2]{1,0:T(2,128)}, u32[]{:S(2)}) copy-start(s32[2,2]{1,0:T(2,128)} %param.16) | copy-start | bytes 52
  47.5 62.3 %all-to-all-start.1 = ((bf16[4,288,1024]{2,1,0:T(8,128)(2,1)}), bf16[4,288,1024]{2,1,0:T(8,128)(2,1)}, u32[]{:S(2)}, u32[]{:S(2)}) async-start(bf16[4,288,1024]{2,1,0:T(8,128)(2,1)} %broadcast_in_dim.76), calls=%async_computation.1 | async-start | bytes 4718592 | tf_op jit(solution)/shard_map/all_to_all | solution.py:48
  103.7 3.1 copy-start.9
  107.9 1.6 slice-start
  108.1 1.5 copy-start.13
  109.6 79.8 %copy-start.1 = (bf16[4,256,512]{2,1,0:T(8,128)(2,1)}, bf16[4,256,512]{2,1,0:T(8,128)(2,1)S(1)}, u32[]{:S(2)}) copy-start(bf16[4,256,512]{2,1,0:T(8,128)(2,1)S(1)} %pad.9.refs_3_.refs_7_.refs_4_) | copy-start | bytes 3145732
  109.8 14.3 %all-to-all-start = ((bf16[4,2,32,2048]{3,2,1,0:T(8,128)(2,1)}), bf16[4,2,32,2048]{3,2,1,0:T(8,128)(2,1)S(1)}, u32[]{:S(2)}, u32[]{:S(2)}) async-start(bf16[4,2,32,2048]{3,2,1,0:T(8,128)(2,1)} %reshape.181), calls=%async_computation | async-start | bytes 2097152 | tf_op jit(solution)/shard_map/all_to_all | solution.py:48
  114.7 10.6 %collective-permute-start = (bf16[4,288,1024]{2,1,0:T(8,128)(2,1)}, bf16[4,288,1024]{2,1,0:T(8,128)(2,1)}, u32[]{:S(2)}, u32[]{:S(2)}) collective-permute-start(bf16[4,288,1024]{2,1,0:T(8,128)(2,1)} %all-to-all-done.1), channel_id=1, source_target_pairs={{0,1},{1,0},{2,3},{3,2},{4,5},{5,4},{6,7},{7,6},{8,9},{9,8},{10,11... | collective-permute-start | bytes 7077896 | tf_op jit(solution)/shard_map/ppermute | solution.py:286
  132.8 5.9 %copy-start = (bf16[4,128,2048]{2,1,0:T(8,128)(2,1)}, bf16[4,128,2048]{2,1,0:T(8,128)(2,1)S(1)}, u32[]{:S(2)}) copy-start(bf16[4,128,2048]{2,1,0:T(8,128)(2,1)S(1)} %slice_dynamic-update-slice_fusion.16.refs_3_.refs_6_.refs_15_.refs_12_) | copy-start | bytes 6291460
  132.9 1.4 copy-start.5
  134.4 1.0 copy-start.7
  135.4 16.2 %copy-start.8 = (bf16[4,1,32,2048]{3,2,1,0:T(8,128)(2,1)S(1)}, bf16[4,1,32,2048]{3,2,1,0:T(8,128)(2,1)}, u32[]{:S(2)}) copy-start(bf16[4,1,32,2048]{3,2,1,0:T(8,128)(2,1)} %get-tuple-element.54) | copy-start | bytes 1572868
  169.9 4.7 %copy-start.3 = (bf16[512,896]{1,0:T(8,128)(2,1)}, bf16[512,896]{1,0:T(8,128)(2,1)S(1)}, u32[]{:S(2)}) copy-start(bf16[512,896]{1,0:T(8,128)(2,1)S(1)} %all-gather.3) | copy-start | bytes 2752516
  189.4 4.7 %copy-start.4 = (bf16[512,896]{1,0:T(8,128)(2,1)}, bf16[512,896]{1,0:T(8,128)(2,1)S(1)}, u32[]{:S(2)}) copy-start(bf16[512,896]{1,0:T(8,128)(2,1)S(1)} %all-gather.4) | copy-start | bytes 2752516
  189.4 19.5 %copy-start.6 = (bf16[4,1,32,2048]{3,2,1,0:T(8,128)(2,1)S(1)}, bf16[4,1,32,2048]{3,2,1,0:T(8,128)(2,1)}, u32[]{:S(2)}) copy-start(bf16[4,1,32,2048]{3,2,1,0:T(8,128)(2,1)} %get-tuple-element.55) | copy-start | bytes 1572868
  215.5 53.7 %collective-permute-start.4 = (bf16[8,176,128]{2,1,0:T(8,128)(2,1)S(1)}, bf16[8,176,128]{2,1,0:T(8,128)(2,1)S(1)}, u32[]{:S(2)}, u32[]{:S(2)}) collective-permute-start(bf16[8,176,128]{2,1,0:T(8,128)(2,1)S(1)} %get-tuple-element.51), channel_id=1, source_target_pairs={{0,1},{1,0},{2,3},{3,2},{4,5},{5,4},{6,7},{7,6},{8,9},{9,8},{10,11... | collective-permute-start | bytes 1081352 | tf_op jit(solution)/shard_map/ppermute | solution.py:429
  233.9 35.3 %collective-permute-start.3 = (bf16[8,176,128]{2,1,0:T(8,128)(2,1)S(1)}, bf16[8,176,128]{2,1,0:T(8,128)(2,1)S(1)}, u32[]{:S(2)}, u32[]{:S(2)}) collective-permute-start(bf16[8,176,128]{2,1,0:T(8,128)(2,1)S(1)} %get-tuple-element.50), channel_id=1, source_target_pairs={{0,1},{1,0},{2,3},{3,2},{4,5},{5,4},{6,7},{7,6},{8,9},{9,8},{10,11... | collective-permute-start | bytes 1081352 | tf_op jit(solution)/shard_map/ppermute | solution.py:429
  247.5 19.9 %copy-start.2 = (bf16[4,256,512]{2,1,0:T(8,128)(2,1)S(1)}, bf16[4,256,512]{2,1,0:T(8,128)(2,1)}, u32[]{:S(2)}) copy-start(bf16[4,256,512]{2,1,0:T(8,128)(2,1)} %copy-done.1) | copy-start | bytes 3145732
  253.9 15.3 %collective-permute-start.2 = (bf16[8,176,128]{2,1,0:T(8,128)(2,1)S(1)}, bf16[8,176,128]{2,1,0:T(8,128)(2,1)S(1)}, u32[]{:S(2)}, u32[]{:S(2)}) collective-permute-start(bf16[8,176,128]{2,1,0:T(8,128)(2,1)S(1)} %get-tuple-element.49), channel_id=1, source_target_pairs={{0,1},{1,0},{2,3},{3,2},{4,5},{5,4},{6,7},{7,6},{8,9},{9,8},{10,11... | collective-permute-start | bytes 1081352 | tf_op jit(solution)/shard_map/ppermute | solution.py:429
  269.1 1.8 collective-permute-start.1
Sparse Core Ops, SparseCore 0:
  10.7 110.6 all-gather.11
